TPU v7x, 32 devices: a whole 2x2x4 slice. The times are simulated.
32 devices in a mesh: freq: 4 (over z), trace: 8 (over y, x, core).
Axes of the slice: x: 2, y: 2, z: 4, core: 2. Of those that a mesh axis runs over, the one named last changes fastest.
Arguments:
- recorded: float32 [8, 2, 2048, 1024], P(None, None, 'freq', 'trace'), may hold values from -16 to 16
- multiples: float32 [8, 2, 2048, 1024], P(None, None, 'freq', 'trace'), may hold values from -6 to 6
Outputs:
- primaries: float32 [8, 2, 2048, 1024], P(None, None, 'freq', 'trace')
- filters: float32 [8, 2, 32, 64], P(None, None, 'freq')
All inputs are finite; a program needn't handle non-finite values.
Results may differ from a plain program's by a relative error of at most 0.0001.
Values sent between devices are 32-bit elements; how exact they have to be, the bound alone decides.
A program may use at most 128 MiB of HBM per device.

v0:
```python
import functools

import jax
import jax.numpy as jnp
from jax import lax
from jax.experimental import pallas as pl
from jax.experimental.pallas import tpu as pltpu
from jax.sharding import PartitionSpec as P

FB = 64
TAPS = 64
ITERS = 3
HALF = TAPS // 2
LANES = 128
ROWS = 4 + HALF
F32 = jnp.float32
BF16 = jnp.bfloat16


def lanes_of(shape):
    return lax.broadcasted_iota(jnp.int32, shape, len(shape) - 1)


def turn(value, shift):
    shift = shift % LANES
    return value if shift == 0 else pltpu.roll(value, shift, 1)


def split(value):
    high = value.astype(BF16)
    return high, (value - high.astype(F32)).astype(BF16)


def tiles(m_ref, left_ref, right_ref, b, part):
    group_rows = left_ref.shape[2]
    group, first = (b * FB) // group_rows, (b * FB) % group_rows
    main = m_ref[0, part, b * FB : (b + 1) * FB, :]
    left = turn(left_ref[0, part, first : first + FB, :], LANES - HALF - HALF * group)
    right = turn(right_ref[0, part, first : first + FB, :], -HALF * group)
    lane = lanes_of(main.shape)
    halo = jnp.where(lane < HALF, right, jnp.where(lane >= LANES - HALF, left, 0.0))
    return main, halo


def three(pair):
    (rh, rl), (ih, il) = pair
    return jnp.concatenate([rh, ih, rh, ih, rl, il], 0)


def three_re(pair):
    (rh, rl), (ih, il) = pair
    return jnp.concatenate([rh, ih, rl, il, rh, ih], 0)


def three_im(pair):
    (rh, rl), (ih, il) = pair
    return jnp.concatenate([ih, -rh, il, -rl, ih, -rh], 0)


def over_first(left, right):
    return lax.dot_general(left, right, (((0,), (0,)), ((), ())), preferred_element_type=F32)


def diagonals(main, halo, offset):
    lane = lanes_of((8, LANES))
    total = jnp.zeros((8, LANES), F32)
    for g in range(LANES // 8):
        shift = offset - 8 * g
        own = turn(main[8 * g : 8 * g + 8], shift)
        other = turn(halo[8 * g : 8 * g + 8], shift)
        outside = lane < shift if shift >= 0 else lane >= LANES + shift
        total = total + jnp.where(outside, other, own)
    row = lax.broadcasted_iota(jnp.int32, (8, LANES), 0)
    result = jnp.where(row == 0, total, 0.0)
    for s in range(1, 8):
        result = result + jnp.where(row == s, turn(total, -s), 0.0)
    return jnp.sum(result, axis=0, keepdims=True)


def stats_kernel(mask_ref, m_ref, left_ref, right_ref, rec_ref, out_ref):
    for b in range(m_ref.shape[2] // FB):
        windows, starts, ends, records = [], [], [], []
        for part in range(2):
            main, halo = tiles(m_ref, left_ref, right_ref, b, part)
            turned = turn(main, HALF)
            shifted = jnp.where(lanes_of(main.shape) < HALF, turn(halo, HALF), turned)
            windows.append(split(jnp.concatenate([main, halo], 1)))
            starts.append(split(jnp.concatenate([shifted, rec_ref[0, part, b * FB : (b + 1) * FB, :]], 1)))
            ends.append(split(turned))
        crossed = over_first(three(starts), jnp.concatenate([three_re(windows), three_im(windows)], 1))
        edge = over_first(three(ends)[:, :TAPS], jnp.concatenate([three_re(ends), three_im(ends)], 1))
        quads = []
        for first, offset in ((0, HALF), (LANES, HALF - 1)):
            for column in (0, 2 * LANES):
                rows = slice(first, first + LANES)
                quads.append(
                    diagonals(
                        crossed[rows, column : column + LANES],
                        crossed[rows, column + LANES : column + 2 * LANES],
                        offset,
                    )
                )
        quads[3] = -quads[3]
        real, imag = edge[:, :LANES], turn(edge[:, LANES:], TAPS)
        lane = lanes_of((HALF, LANES))
        corner = jnp.where(
            lane < HALF,
            real[:HALF],
            jnp.where(lane < TAPS, real[HALF:], jnp.where(lane < TAPS + HALF, imag[:HALF], imag[HALF:])),
        )
        corner = jnp.where(mask_ref[...] > 0.0, corner, 0.0)
        out_ref[0, :, b, :] = jnp.concatenate(quads + [corner], 0)


def exact(left, right):
    return jnp.dot(left, right, precision=lax.Precision.HIGHEST, preferred_element_type=F32)


def mirror(total):
    rows = lax.broadcasted_iota(jnp.int32, (LANES, LANES), 0)
    return (rows + lanes_of((LANES, LANES)) == total).astype(F32)


def total_of(value):
    return jnp.sum(jnp.sum(value, axis=1, keepdims=True), axis=0, keepdims=True)


def solve_kernel(weight, st_ref, out_ref, matrix):
    blocks = st_ref.shape[0] * st_ref.shape[3]

    def row(r):
        return st_ref[:, 0, r, :, :].reshape(blocks, LANES)

    lane = lanes_of((blocks, LANES))
    place = lane % TAPS
    is_real = lane < TAPS
    carry_right = place < HALF - 1
    carry_left = place > HALF
    in_right = place < HALF
    right = [None] * HALF
    for i in reversed(range(HALF)):
        value = jnp.where(in_right, row(4 + i), 0.0)
        if i + 1 < HALF:
            value = value + jnp.where(carry_right, turn(right[i + 1], -1), 0.0)
        right[i] = value
        if i >= 1:
            matrix[i - 1] = jnp.where(carry_right, turn(value, -1), 0.0)
    matrix[HALF - 1] = jnp.zeros((blocks, LANES), F32)
    last = None
    for i in range(HALF):
        value = jnp.where(in_right, 0.0, row(4 + i))
        if i:
            value = value + jnp.where(carry_left, turn(last, 1), 0.0)
        last = value
        matrix[HALF + i] = value
    lag_real = jnp.where(is_real, row(0), 0.0) + jnp.where(lane < HALF, right[0], 0.0)
    lag_imag = jnp.where(is_real, row(1), 0.0) + jnp.where(lane < HALF, turn(right[0], TAPS), 0.0)
    back = mirror(LANES)
    toep_real = jnp.where(is_real, lag_real, exact(lag_real, back))
    toep_imag = jnp.where(is_real, -lag_imag, exact(lag_imag, back))
    for t in range(TAPS):
        toep = jnp.where(is_real, turn(toep_real, t), turn(toep_imag, TAPS + t))
        matrix[t] = toep - jnp.where(is_real, matrix[t], -matrix[t])

    gradient = jnp.where(is_real, row(2), turn(row(3), TAPS))
    filters = jnp.zeros((blocks, LANES), F32)
    direction = norm_now = None
    none = jnp.zeros((1, LANES), F32)
    for iteration in range(ITERS):
        norm_next = total_of(gradient * gradient)
        if iteration == 0:
            direction = gradient
        else:
            direction = gradient + (norm_next / norm_now) * direction
        norm_now = norm_next
        by_real = jnp.zeros((blocks, LANES), F32)
        by_imag = jnp.zeros((blocks, LANES), F32)
        for t in range(TAPS):
            by_real = by_real + direction[:, t : t + 1] * matrix[t]
            by_imag = by_imag + direction[:, TAPS + t : TAPS + t + 1] * matrix[t]
        by_imag = turn(by_imag, TAPS)
        normal = by_real + jnp.where(is_real, -by_imag, by_imag)
        before = jnp.concatenate([none, direction[:-1]], 0)
        after = jnp.concatenate([direction[1:], none], 0)
        normal = normal + weight * (2.0 * direction - before - after)
        step_len = norm_now / total_of(direction * normal)
        filters = filters + step_len * direction
        gradient = gradient - step_len * normal
    out_ref[0, 0] = exact(filters, mirror(TAPS - 1))
    out_ref[0, 1] = exact(jnp.where(is_real, 0.0, filters), mirror(2 * TAPS - 1))


def forward_kernel(h_ref, m_ref, left_ref, right_ref, rec_ref, out_ref):
    rows = lax.broadcasted_iota(jnp.int32, (LANES, LANES), 0)
    tap = lanes_of((LANES, LANES)) + HALF - rows
    direct = (tap >= 0) & (tap < TAPS)
    for b in range(m_ref.shape[2] // FB):
        windows, bands = [], []
        for part in range(2):
            windows.append(split(jnp.concatenate(tiles(m_ref, left_ref, right_ref, b, part), 1)))
            base = jnp.where(lanes_of((1, LANES)) < TAPS, h_ref[0, part, b : b + 1, :], 0.0)
            base = pltpu.roll(jnp.broadcast_to(base, (8, LANES)), 0, 1, stride=1, stride_axis=0)
            ring = jnp.concatenate([turn(base, 8 * g - HALF) for g in range(LANES // 8)], 0)
            band = jnp.concatenate([jnp.where(direct, ring, 0.0), jnp.where(direct, 0.0, ring)], 0)
            bands.append(split(band))
        (rh, rl), (ih, il) = windows
        high, low = jnp.concatenate([rh, ih], 1), jnp.concatenate([rl, il], 1)
        sides = []
        for term in range(2):
            real, imag = bands[0][term], bands[1][term]
            sides.append(
                jnp.concatenate(
                    [jnp.concatenate([real, imag], 1), jnp.concatenate([-imag, real], 1)], 0
                )
            )
        both = jnp.dot(jnp.concatenate([high, low], 0), sides[0], preferred_element_type=F32)
        applied = both[:FB] + both[FB:] + jnp.dot(high, sides[1], preferred_element_type=F32)
        span = slice(b * FB, (b + 1) * FB)
        out_ref[0, 0, span, :] = rec_ref[0, 0, span, :] - applied[:, :LANES]
        out_ref[0, 1, span, :] = rec_ref[0, 1, span, :] - applied[:, LANES:]


def packed(value):
    count = LANES // HALF
    return jnp.concatenate(jnp.split(value, count, axis=2), axis=3)


def body(recorded, multiples):
    shots, parts, freq_rows, trace_rows = multiples.shape
    blocks = freq_rows // FB
    trace_count, freq_count = lax.axis_size("trace"), lax.axis_size("freq")
    me = lax.axis_index("trace")
    up = [(i, i + 1) for i in range(trace_count - 1)]
    down = [(j, i) for i, j in up]
    left = lax.ppermute(packed(multiples[..., trace_rows - HALF :]), "trace", up)
    right = lax.ppermute(packed(multiples[..., :HALF]), "trace", down)

    place = jnp.arange(LANES)[None, :] % TAPS < HALF
    mask = jnp.where(place, me == trace_count - 1, me == 0).astype(F32)

    field = pl.BlockSpec((1, parts, freq_rows, trace_rows), lambda s: (s, 0, 0, 0))
    side = pl.BlockSpec((1, parts) + left.shape[2:], lambda s: (s, 0, 0, 0))
    stats = pl.pallas_call(
        stats_kernel,
        grid=(shots,),
        in_specs=[pl.BlockSpec((1, LANES), lambda s: (0, 0)), field, side, side, field],
        out_specs=pl.BlockSpec((1, ROWS, blocks, LANES), lambda s: (s, 0, 0, 0)),
        out_shape=jax.ShapeDtypeStruct((shots, ROWS, blocks, LANES), F32),
        name="stats",
    )(mask, multiples, left, right, recorded)

    per_device = -(-shots // trace_count)
    extra = per_device * trace_count - shots
    if extra:
        stats = jnp.pad(stats, ((0, extra), (0, 0), (0, 0), (0, 0)))
    stats = lax.all_to_all(stats, "trace", split_axis=0, concat_axis=0, tiled=True)
    stats = jnp.sum(stats.reshape((trace_count, per_device) + stats.shape[1:]), axis=0)
    stats = lax.all_gather(stats, "freq", axis=0)

    weight = 0.5 * FB * trace_rows * trace_count
    all_blocks = blocks * freq_count
    solved = pl.pallas_call(
        functools.partial(solve_kernel, weight),
        grid=(per_device,),
        in_specs=[pl.BlockSpec((freq_count, 1, ROWS, blocks, LANES), lambda s: (0, s, 0, 0, 0))],
        out_specs=pl.BlockSpec((1, parts, all_blocks, LANES), lambda s: (s, 0, 0, 0)),
        out_shape=jax.ShapeDtypeStruct((per_device, parts, all_blocks, LANES), F32),
        scratch_shapes=[pltpu.VMEM((TAPS, all_blocks, LANES), F32)],
        name="solve",
    )(stats)
    mine = lax.dynamic_slice_in_dim(solved, lax.axis_index("freq") * blocks, blocks, axis=2)
    taps = lax.all_gather(mine, "trace", axis=0, tiled=True)[:shots]

    primaries = pl.pallas_call(
        forward_kernel,
        grid=(shots,),
        in_specs=[pl.BlockSpec((1, parts, blocks, LANES), lambda s: (s, 0, 0, 0)), field, side, side, field],
        out_specs=field,
        out_shape=jax.ShapeDtypeStruct(recorded.shape, F32),
        name="forward",
    )(taps, multiples, left, right, recorded)
    return primaries, taps[..., :TAPS]


def solution(mesh):
    spec = P(None, None, "freq", "trace")
    return jax.shard_map(
        body,
        mesh=mesh,
        in_specs=(spec, spec),
        out_specs=(spec, P(None, None, "freq", None)),
        check_vma=False,
    )
```

profile of v0, /device:TPU:0, one launch (start us, length us, event | category | flops | bytes accessed | tf_op | source)
XLA Modules:
  0.0 151.7 jit_solution(10081131332256860243)
XLA Ops:
  0.6 5.0 %fusion = (f32[8,2,128,32]{3,2,1,0:T(8,128)S(1)}, f32[8,2,128,32]{3,2,1,0:T(8,128)S(1)}, f32[8,2,128,32]{3,2,1,0:T(8,128)S(1)}, f32[8,2,128,32]{3,2,1,0:T(8,128)...) fusion(f32[8,2,512,128]{3,2,1,0:T(8,128)} %m_ref.3), kind=kLoop, calls=%fused_computation.5 | loop fusion | bytes 4194304 | tf_op jit(solution)/shard_map/split | solution.py:225
  5.6 0.9 pad_maximum_fusion.1
  6.5 1.3 collective-permute-start.1
  7.8 1.9 %pad_maximum_fusion = f32[8,2,128,128]{3,2,1,0:T(8,128)} fusion(f32[8,2,128,32]{3,2,1,0:T(8,128)S(1)} %get-tuple-element.6, f32[8,2,128,32]{3,2,1,0:T(8,128)S(1)} %get-tuple-element.7, f32[8,2,128,32]{3,2,1,0:T(8,128)S(1)} %get-tuple-element.8, f32[8,2,128,32]{3,2,1,0:T(8,128)S(1)} %get-tuple-element.9), kind=kLoop, calls=%fused_computation | loop fusion | flops 786432 | bytes 2097152 | tf_op jit(solution)/shard_map/concatenate | solution.py:225
  9.6 3.1 %collective-permute-start = (f32[8,2,128,128]{3,2,1,0:T(8,128)}, f32[8,2,128,128]{3,2,1,0:T(8,128)S(1)}, u32[]{:S(2)}, u32[]{:S(2)}) collective-permute-start(f32[8,2,128,128]{3,2,1,0:T(8,128)} %pad_maximum_fusion), channel_id=1, source_target_pairs={{0,1},{1,2},{2,3},{3,4},{4,5},{5,6},{6,7},{8,9},{9,10},{10,11},{11... | collective-permute-start | bytes 3145736 | tf_op jit(solution)/shard_map/ppermute | solution.py:235
  12.7 0.5 select_convert_fusion.mask_ref
  13.3 0.0 collective-permute-done.1.right_ref
  13.3 0.0 copy-start
  13.3 1.9 %collective-permute-done.left_ref = f32[8,2,128,128]{3,2,1,0:T(8,128)S(1)} collective-permute-done((f32[8,2,128,128]{3,2,1,0:T(8,128)}, f32[8,2,128,128]{3,2,1,0:T(8,128)S(1)}, u32[]{:S(2)}, u32[]{:S(2)}) %collective-permute-start) | collective-permute-done | bytes 1048608 | tf_op jit(solution)/shard_map/ppermute | solution.py:235
  15.2 0.0 copy-done
  15.2 0.0 copy-start.1
  15.2 1.0 copy-done.1
  16.1 46.6 %stats.1 = f32[8,36,8,128]{3,2,1,0:T(8,128)} custom-call(f32[1,128]{1,0:T(1,128)} %select_convert_fusion.mask_ref, f32[8,2,512,128]{3,2,1,0:T(8,128)} %m_ref.3, f32[8,2,128,128]{3,2,1,0:T(8,128)} %copy-done.1, f32[8,2,128,128]{3,2,1,0:T(8,128)} %copy-done, f32[8,2,512,128]{3,2,1,0:T(8,128)} %rec_ref.3), custom_call_target="tpu_custom_call" | custom-call | tf_op jit(solution)/shard_map/stats/pallas_call | solution.py:243
  62.7 23.8 %all-to-all-start = ((f32[8,36,8,128]{3,2,1,0:T(8,128)}), f32[8,36,8,128]{3,2,1,0:T(8,128)S(1)}, u32[]{:S(2)}, u32[]{:S(2)}) async-start(f32[8,36,8,128]{3,2,1,0:T(8,128)} %stats.1), calls=%async_computation | async-start | bytes 2359296 | tf_op jit(solution)/shard_map/all_to_all | solution.py:256
  86.5 16.8 %all-to-all-done = f32[8,36,8,128]{3,2,1,0:T(8,128)S(1)} async-done(((f32[8,36,8,128]{3,2,1,0:T(8,128)}), f32[8,36,8,128]{3,2,1,0:T(8,128)S(1)}, u32[]{:S(2)}, u32[]{:S(2)}) %all-to-all-start) | async-done | bytes 1179680 | tf_op jit(solution)/shard_map/all_to_all | solution.py:256
  103.3 0.1 reduce_sum.9
  103.4 17.3 %all-gather = f32[144,8,128]{2,1,0:T(8,128)} all-gather(f32[36,8,128]{2,1,0:T(8,128)S(1)} %reduce_sum.9), channel_id=2, replica_groups=mesh['freq'=4,'trace'=8] {'freq'}, dimensions={0}, use_global_device_ids=true | all-gather | bytes 737280 | tf_op jit(solution)/shard_map/all_gather | solution.py:258
  120.7 7.4 %solve.1 = f32[1,2,32,128]{3,2,1,0:T(8,128)} custom-call(f32[4,1,36,8,128]{4,3,2,1,0:T(8,128)} %bitcast.2), custom_call_target="tpu_custom_call" | custom-call | tf_op jit(solution)/shard_map/solve/pallas_call | solution.py:262
  128.1 0.7 constant_dynamic-slice_fusion
  128.8 9.2 %all_gather.11.h_ref = f32[8,2,8,128]{3,2,1,0:T(8,128)} all-gather(f32[1,2,8,128]{3,2,1,0:T(8,128)S(1)} %constant_dynamic-slice_fusion), channel_id=1, replica_groups=mesh['freq'=4,'trace'=8] {'trace'}, dimensions={0}, use_global_device_ids=true | all-gather | bytes 73728 | tf_op jit(solution)/shard_map/all_gather | solution.py:272
  138.0 0.0 copy-start.2
  138.0 13.0 %forward.1 = f32[8,2,512,128]{3,2,1,0:T(8,128)} custom-call(f32[8,2,8,128]{3,2,1,0:T(8,128)} %all_gather.11.h_ref, f32[8,2,512,128]{3,2,1,0:T(8,128)} %m_ref.3, f32[8,2,128,128]{3,2,1,0:T(8,128)} %copy-done.1, f32[8,2,128,128]{3,2,1,0:T(8,128)} %copy-done, f32[8,2,512,128]{3,2,1,0:T(8,128)} %rec_ref.3), custom_call_target="tpu_custom_call" | custom-call | tf_op jit(solution)/shard_map/forward/pallas_call | solution.py:274
  151.0 0.0 copy-done.2
  151.0 0.6 copy.5
Async XLA Ops:
  6.5 6.8 %collective-permute-start.1 = (f32[8,2,128,128]{3,2,1,0:T(8,128)S(1)}, f32[8,2,128,128]{3,2,1,0:T(8,128)S(1)}, u32[]{:S(2)}, u32[]{:S(2)}) collective-permute-start(f32[8,2,128,128]{3,2,1,0:T(8,128)S(1)} %pad_maximum_fusion.1), channel_id=1, source_target_pairs={{1,0},{2,1},{3,2},{4,3},{5,4},{6,5},{7,6},{9,8},{10,9},{11,10},{12... | collective-permute-start | bytes 3145736 | tf_op jit(solution)/shard_map/ppermute | solution.py:236
  9.6 5.5 %collective-permute-start = (f32[8,2,128,128]{3,2,1,0:T(8,128)}, f32[8,2,128,128]{3,2,1,0:T(8,128)S(1)}, u32[]{:S(2)}, u32[]{:S(2)}) collective-permute-start(f32[8,2,128,128]{3,2,1,0:T(8,128)} %pad_maximum_fusion), channel_id=1, source_target_pairs={{0,1},{1,2},{2,3},{3,4},{4,5},{5,6},{6,7},{8,9},{9,10},{10,11},{11... | collective-permute-start | bytes 3145736 | tf_op jit(solution)/shard_map/ppermute | solution.py:235
  13.3 1.9 %copy-start = (f32[8,2,128,128]{3,2,1,0:T(8,128)}, f32[8,2,128,128]{3,2,1,0:T(8,128)S(1)}, u32[]{:S(2)}) copy-start(f32[8,2,128,128]{3,2,1,0:T(8,128)S(1)} %collective-permute-done.1.right_ref) | copy-start | bytes 3145732
  15.2 1.0 copy-start.1
  62.7 40.6 %all-to-all-start = ((f32[8,36,8,128]{3,2,1,0:T(8,128)}), f32[8,36,8,128]{3,2,1,0:T(8,128)S(1)}, u32[]{:S(2)}, u32[]{:S(2)}) async-start(f32[8,36,8,128]{3,2,1,0:T(8,128)} %stats.1), calls=%async_computation | async-start | bytes 2359296 | tf_op jit(solution)/shard_map/all_to_all | solution.py:256
  138.0 13.0 %copy-start.2 = (f32[8,2,8,128]{3,2,1,0:T(8,128)S(1)}, f32[8,2,8,128]{3,2,1,0:T(8,128)}, u32[]{:S(2)}) copy-start(f32[8,2,8,128]{3,2,1,0:T(8,128)} %all_gather.11.h_ref) | copy-start | bytes 196612
where the time goes:
time: 152 us
  Pallas kernels  67 us (44%)
  starting transfers between devices  28.2 us (19%)
  blocking collectives  26.5 us (17%)
  waiting for transfers between devices  18.7 us (12%)
  local copies, waits for them, and re-layouts  7.28 us (5%)
  other arithmetic  3.31 us (2%)
    pallas_call x1, Pallas kernels, body(): pl.pallas_call(stats_kernel, grid=(shots,), in_specs=[pl.BlockSpec((1, LA...  46.6 us
    all_to_all x1, starting transfers between devices, body(): lax.all_to_all(stats, 'trace', split_axis=0, concat_axis=0, tiled=True)  23.8 us
    all_gather x1, blocking collectives, body(): stats = lax.all_gather(stats, 'freq', axis=0)  17.3 us
    all_to_all x1, waiting for transfers between devices, body(): lax.all_to_all(stats, 'trace', split_axis=0, concat_axis=0, tiled=True)  16.8 us
    pallas_call x1, Pallas kernels, body(): pl.pallas_call(forward_kernel, grid=(shots,), in_specs=[pl.BlockSpec((1,...  13 us
    all_gather x1, blocking collectives, body(): taps = lax.all_gather(mine, 'trace', axis=0, tiled=True)[:shots]  9.22 us
    pallas_call x1, Pallas kernels, body(): pl.pallas_call(functools.partial(solve_kernel, weight), grid=(per_device,...  7.39 us
    split x1, local copies, waits for them, and re-layouts, packed(): return jnp.concatenate(jnp.split(value, count, axis=2), axis=3)  4.97 us
  transfers between devices with their start and end apart: 3, of which 2 were waited for; matrix products, arithmetic and copies ran while one was open for 2% of the time, Pallas kernels for 0%

commit v1 on v0

v1 whole, which is shorter than its diff:
```python
import functools

import jax
import jax.numpy as jnp
import numpy as np
from jax import lax
from jax.experimental import pallas as pl
from jax.experimental.pallas import tpu as pltpu
from jax.sharding import PartitionSpec as P

FB = 64
TAPS = 64
ITERS = 3
HALF = TAPS // 2
LANES = 128
POINTS = 2 * LANES
F32 = jnp.float32
BF16 = jnp.bfloat16
MESH = pl.DeviceIdType.MESH


def lanes_of(shape):
    return lax.broadcasted_iota(jnp.int32, shape, len(shape) - 1)


def turn(value, shift):
    shift = shift % LANES
    return value if shift == 0 else pltpu.roll(value, shift, 1)


def split(value):
    high = value.astype(BF16)
    return high, (value - high.astype(F32)).astype(BF16)


def waves(positions):
    phase = (2 * np.pi / POINTS) * np.outer(np.asarray(positions), np.arange(LANES) + 0.5)
    return np.cos(phase), np.sin(phase)


def both_waves(positions):
    return np.concatenate(waves(positions), 1)


def halves(table):
    high = table.astype(np.float32).astype(BF16)
    return high, (table - high.astype(np.float64)).astype(np.float32).astype(BF16)


def fit_tables():
    high, low = halves(both_waves(np.arange(LANES)))
    tail_high, tail_low = halves(both_waves(LANES + np.arange(TAPS)))
    tail = np.concatenate([tail_high, tail_high, tail_low, np.zeros_like(tail_low)], 0)
    lag_cos, lag_sin = waves(np.arange(TAPS))
    none = np.zeros((LANES, TAPS))
    lags = np.block([[lag_cos.T, none], [none, 2.0 * lag_sin.T]]) / LANES
    right = both_waves(-1 - np.arange(TAPS)).T
    none = np.zeros_like(right)
    sides = np.block([[right, none], [none, right]]) / LANES
    return (
        np.concatenate([high, high], 0),
        low,
        tail,
        lags.astype(np.float32),
        sides.astype(np.float32),
    )


def forward_tables():
    taps = both_waves(np.arange(TAPS))
    none = np.zeros_like(taps)
    high, low = halves(np.block([[taps, none], [none, taps]]))
    back = halves(both_waves(TAPS + np.arange(LANES)).T / LANES)
    return np.concatenate([high, high], 0), low, np.concatenate(back, 1)


def three(pair):
    (rh, rl), (ih, il) = pair
    return jnp.concatenate([rh, ih, rh, ih, rl, il], 0)


def three_re(pair):
    (rh, rl), (ih, il) = pair
    return jnp.concatenate([rh, ih, rl, il, rh, ih], 0)


def three_im(pair):
    (rh, rl), (ih, il) = pair
    return jnp.concatenate([ih, -rh, il, -rl, ih, -rh], 0)


def over_first(left, right):
    return lax.dot_general(left, right, (((0,), (0,)), ((), ())), preferred_element_type=F32)


def product(left, right):
    return jnp.dot(left, right, preferred_element_type=F32)


def exact(left, right):
    return jnp.dot(left, right, precision=lax.Precision.HIGHEST, preferred_element_type=F32)


def mirror(total):
    rows = lax.broadcasted_iota(jnp.int32, (LANES, LANES), 0)
    return (rows + lanes_of((LANES, LANES)) == total).astype(F32)


def total_of(value):
    return jnp.sum(jnp.sum(value, axis=1, keepdims=True), axis=0, keepdims=True)


def column_sum(value):
    return jnp.sum(value, axis=0, keepdims=True)


def pack_edges(m, edge, s):
    freq_rows = m.shape[2]
    groups = LANES // HALF
    rows = freq_rows // groups
    lane = lanes_of((rows, LANES))
    for part in range(2):
        for side in range(2):
            packed = None
            for g in range(groups):
                shift = HALF * g + HALF if side == 0 else HALF * g
                value = turn(m[s, part, g * rows : (g + 1) * rows, :], shift)
                packed = value if packed is None else jnp.where(lane >= HALF * g, value, packed)
            edge[side, s, part] = packed


def corners(m, corner, s, keep):
    for b in range(m.shape[2] // FB):
        ends = [split(turn(m[s, part, b * FB : (b + 1) * FB, :], HALF)) for part in range(2)]
        edge = over_first(three(ends)[:, :TAPS], jnp.concatenate([three_re(ends), three_im(ends)], 1))
        real, imag = edge[:, :LANES], turn(edge[:, LANES:], TAPS)
        lane = lanes_of((HALF, LANES))
        value = jnp.where(
            lane < HALF,
            real[:HALF],
            jnp.where(lane < TAPS, real[HALF:], jnp.where(lane < TAPS + HALF, imag[:HALF], imag[HALF:])),
        )
        corner[s, :, b, :] = jnp.where(keep, value, 0.0)


def statistics(m, rec, halo, spec, sums, wide, low, tail, s):
    freq_rows = m.shape[2]
    group_rows = freq_rows * HALF // LANES
    lane = lanes_of((FB, LANES))
    for b in range(freq_rows // FB):
        rows = slice(b * FB, (b + 1) * FB)
        group, first = (b * FB) // group_rows, (b * FB) % group_rows
        near = slice(first, first + FB)
        starts, tails = [], []
        for part in range(2):
            turned = turn(m[s, part, rows, :], HALF)
            left = turn(halo[0, s, part, near, :], -HALF * group)
            right = turn(halo[1, s, part, near, :], HALF - HALF * group)
            starts.append(jnp.where(lane < HALF, left, turned))
            tails.append(jnp.where(lane < HALF, turned, right))
        high, rest = split(jnp.concatenate(starts + [rec[s, 0, rows, :], rec[s, 1, rows, :]], 0))
        main = product(jnp.concatenate([high, rest], 1), wide[...]) + product(high, low[...])
        ends = jnp.concatenate(tails, 0)
        top = ends.astype(BF16)
        mixed = jnp.where(
            lanes_of(ends.shape) < TAPS, ends, turn(ends - top.astype(F32), TAPS)
        ).astype(BF16)
        last = product(jnp.concatenate([mixed, top], 1), tail[...])

        def parts(value, first):
            return value[first : first + FB, :LANES], value[first : first + FB, LANES:]

        s_all = parts(main, 0) + parts(main, FB)
        t_all = parts(last, 0) + parts(last, FB)
        r_ac, r_as, r_bc, r_bs = parts(main, 2 * FB) + parts(main, 3 * FB)
        w_all = [x + y for x, y in zip(s_all, t_all)]
        for i in range(4):
            spec[s, i, rows, :] = w_all[i]
        w_ac, w_as, w_bc, w_bs = w_all
        t_ac, t_as, t_bc, t_bs = t_all
        power = sum(x * (w + t) for x, w, t in zip(s_all, w_all, t_all))
        cross = (w_ac * w_bs - w_as * w_bc) - (t_ac * t_bs - t_as * t_bc)
        found = [
            power,
            cross,
            w_ac * r_ac + w_as * r_as + w_bc * r_bc + w_bs * r_bs,
            w_ac * r_as - w_as * r_ac + w_bc * r_bs - w_bs * r_bc,
            w_ac * r_bc + w_as * r_bs - w_bc * r_ac - w_bs * r_as,
            w_ac * r_bs - w_as * r_bc - w_bc * r_as + w_bs * r_ac,
        ]
        for i in range(6):
            sums[i, s, b : b + 1, :] = column_sum(found[i])


def prepare_corners(corner, matrix, slot):
    blocks = corner.shape[0] * corner.shape[3]

    def row(r):
        return corner[:, slot, r, :, :].reshape(blocks, LANES)

    lane = lanes_of((blocks, LANES))
    place = lane % TAPS
    carry_right = place < HALF - 1
    carry_left = place > HALF
    in_right = place < HALF
    right = None
    for i in reversed(range(HALF)):
        value = jnp.where(in_right, row(i), 0.0)
        if right is not None:
            value = value + jnp.where(carry_right, turn(right, -1), 0.0)
        right = value
        if i >= 1:
            matrix[i - 1] = jnp.where(carry_right, turn(value, -1), 0.0)
    matrix[HALF - 1] = jnp.zeros((blocks, LANES), F32)
    last = None
    for i in range(HALF):
        value = jnp.where(in_right, 0.0, row(i))
        if i:
            value = value + jnp.where(carry_left, turn(last, 1), 0.0)
        last = value
        matrix[HALF + i] = value
    matrix[TAPS] = right


def solve(weight, lag, gradient, matrix):
    blocks = lag.shape[0]
    lane = lanes_of((blocks, LANES))
    is_real = lane < TAPS
    right = matrix[TAPS]
    lag_real = jnp.where(is_real, lag, 0.0) + jnp.where(lane < HALF, right, 0.0)
    lag_imag = jnp.where(is_real, turn(lag, TAPS), 0.0) + jnp.where(lane < HALF, turn(right, TAPS), 0.0)
    back = mirror(LANES)
    toep_real = jnp.where(is_real, lag_real, exact(lag_real, back))
    toep_imag = jnp.where(is_real, -lag_imag, exact(lag_imag, back))
    for t in range(TAPS):
        toep = jnp.where(is_real, turn(toep_real, t), turn(toep_imag, TAPS + t))
        matrix[t] = toep - jnp.where(is_real, matrix[t], -matrix[t])

    filters = jnp.zeros((blocks, LANES), F32)
    direction = norm_now = None
    none = jnp.zeros((1, LANES), F32)
    for iteration in range(ITERS):
        norm_next = total_of(gradient * gradient)
        if iteration == 0:
            direction = gradient
        else:
            direction = gradient + (norm_next / norm_now) * direction
        norm_now = norm_next
        by_real = jnp.zeros((blocks, LANES), F32)
        by_imag = jnp.zeros((blocks, LANES), F32)
        for t in range(TAPS):
            by_real = by_real + direction[:, t : t + 1] * matrix[t]
            by_imag = by_imag + direction[:, TAPS + t : TAPS + t + 1] * matrix[t]
        by_imag = turn(by_imag, TAPS)
        normal = by_real + jnp.where(is_real, -by_imag, by_imag)
        before = jnp.concatenate([none, direction[:-1]], 0)
        after = jnp.concatenate([direction[1:], none], 0)
        normal = normal + weight * (2.0 * direction - before - after)
        step_len = norm_now / total_of(direction * normal)
        filters = filters + step_len * direction
        gradient = gradient - step_len * normal
    rows = lax.broadcasted_iota(jnp.int32, (LANES, LANES), 0)
    columns = lanes_of((LANES, LANES))
    flip = (rows + columns == jnp.where(columns < TAPS, TAPS - 1, 3 * TAPS - 1)).astype(F32)
    return exact(filters, flip)


def fit_kernel(
    weight,
    trace_count,
    freq_count,
    per_device,
    relay_at,
    m_any,
    rec_any,
    wide,
    low,
    tail,
    lags,
    sides,
    taps_out,
    spec_any,
    m,
    rec,
    edge,
    halo,
    spec,
    sums,
    corner,
    corner_in,
    corner_all,
    stats,
    stats_in,
    stats_all,
    taps,
    solved,
    matrix,
    m_sem,
    rec_sem,
    spec_sem,
    edge_send,
    halo_sem,
    corner_send,
    corner_sem,
    relay_send,
    relay_sem,
    stats_send,
    stats_sem,
    gather_send,
    gather_sem,
    taps_send,
    taps_sem,
):
    shots = m.shape[0]
    blocks = m.shape[2] // FB
    owners = -(-shots // per_device)
    last = trace_count - 1
    me = lax.axis_index("trace")
    layer = lax.axis_index("freq")
    at_edge = (me == 0) | (me == last)
    owns = me < owners

    def remote(source, target, send, arrive, **where):
        return pltpu.make_async_remote_copy(
            src_ref=source,
            dst_ref=target,
            send_sem=send,
            recv_sem=arrive,
            device_id=where,
            device_id_type=MESH,
        )

    def load(source, target, sem, s):
        return pltpu.make_async_copy(source.at[s], target.at[s], sem.at[s])

    for s in range(shots):
        load(m_any, m, m_sem, s).start()
    for s in range(shots):
        load(rec_any, rec, rec_sem, s).start()

    barrier = pltpu.get_barrier_semaphore()
    for o in range(1, trace_count):
        pl.semaphore_signal(
            barrier, inc=1, device_id={"trace": lax.rem(me + o, trace_count)}, device_id_type=MESH
        )
    for o in range(1, freq_count):
        pl.semaphore_signal(
            barrier, inc=1, device_id={"freq": lax.rem(layer + o, freq_count)}, device_id_type=MESH
        )
    pl.semaphore_wait(barrier, trace_count + freq_count - 2)

    def halo_copy(side, s):
        other = jnp.minimum(me + 1, last) if side == 0 else jnp.maximum(me - 1, 0)
        return remote(
            edge.at[side, s], halo.at[side, s], edge_send.at[side, s], halo_sem.at[side, s], trace=other
        )

    sends = (me < last, me > 0)
    receives = (me > 0, me < last)

    @pl.when(me == 0)
    def _():
        halo[0] = jnp.zeros(halo.shape[1:], F32)

    @pl.when(me == last)
    def _():
        halo[1] = jnp.zeros(halo.shape[1:], F32)

    def send_edges(s, carry):
        load(m_any, m, m_sem, s).wait()
        pack_edges(m, edge, s)
        for side in range(2):

            @pl.when(sends[side])
            def _():
                halo_copy(side, s).start()

        return carry

    lax.fori_loop(0, shots, send_edges, 0)

    def corner_copy(end, s, owner, slot):
        return remote(
            corner.at[s], corner_in.at[end, slot], corner_send.at[s], corner_sem.at[end, slot], trace=owner
        )

    place = lanes_of((HALF, LANES)) % TAPS < HALF
    keep = (place & (me == last)) | (jnp.logical_not(place) & (me == 0))

    @pl.when(at_edge)
    def _():
        def fill(s, carry):
            corners(m, corner, s, keep)
            owner, slot = s // per_device, s % per_device
            for end, where in ((0, 0), (1, last)):

                @pl.when((me == where) & (owner != where))
                def _():
                    corner_copy(end, s, owner, slot).start()

                @pl.when((me == where) & (owner == where))
                def _():
                    corner_in[end, slot] = corner[s]

            return carry

        lax.fori_loop(0, shots, fill, 0)

    def relay_copy(o):
        return remote(
            corner_all.at[layer],
            corner_all.at[layer],
            relay_send.at[o],
            relay_sem.at[layer],
            freq=lax.rem(layer + o, freq_count),
        )

    def relay():
        for slot in range(per_device):
            for end, where in ((0, 0), (1, last)):

                @pl.when(me != where)
                def _():
                    corner_copy(end, 0, me, slot).wait_recv()

            corner_all[layer, slot] = corner_in[0, slot] + corner_in[1, slot]
        for o in range(1, freq_count):
            relay_copy(o).start()

    def measure(s, carry):
        load(rec_any, rec, rec_sem, s).wait()
        for side in range(2):

            @pl.when(receives[side])
            def _():
                halo_copy(side, s).wait_recv()

        statistics(m, rec, halo, spec, sums, wide, low, tail, s)
        pltpu.make_async_copy(spec.at[s], spec_any.at[s], spec_sem.at[s]).start()

        @pl.when((s == relay_at) & owns)
        def _():
            relay()

        return carry

    lax.fori_loop(0, shots, measure, 0)

    def flat(i):
        return sums[i].reshape(shots * blocks, LANES)

    lag = exact(jnp.concatenate([flat(0), flat(1)], 1), lags[...])
    side = exact(jnp.concatenate([flat(i) for i in range(2, 6)], 1), sides[...])
    stats[:, 0] = lag.reshape(shots, blocks, LANES)
    stats[:, 1] = side.reshape(shots, blocks, LANES)

    def stats_copy(s):
        return remote(
            stats.at[s],
            stats_in.at[me, s % per_device],
            stats_send.at[s],
            stats_sem.at[me, s % per_device],
            trace=s // per_device,
        )

    for s in range(shots):

        @pl.when(me != s // per_device)
        def _():
            stats_copy(s).start()

    def gather_copy(o):
        return remote(
            stats_all.at[layer],
            stats_all.at[layer],
            gather_send.at[o],
            gather_sem.at[layer],
            freq=lax.rem(layer + o, freq_count),
        )

    def taps_copy(o):
        own = pl.ds(me * per_device, per_device)
        return remote(
            taps.at[own], taps.at[own], taps_send.at[o], taps_sem.at[me], trace=lax.rem(me + o, trace_count)
        )

    def solve_own():
        for o in range(1, freq_count):
            other = lax.rem(layer + o, freq_count)
            remote(
                corner_all.at[other], corner_all.at[other], relay_send.at[o], relay_sem.at[other], freq=other
            ).wait_recv()
        for slot in range(per_device):
            prepare_corners(corner_all, matrix.at[slot], slot)
        for slot in range(per_device):
            whole = stats[me * per_device + slot]
            for o in range(1, trace_count):
                other = lax.rem(me + o, trace_count)
                remote(
                    stats.at[slot],
                    stats_in.at[other, slot],
                    stats_send.at[slot],
                    stats_sem.at[other, slot],
                    trace=other,
                ).wait_recv()
                whole = whole + stats_in[other, slot]
            stats_all[layer, slot] = whole
        for o in range(1, freq_count):
            gather_copy(o).start()
        for o in range(1, freq_count):
            other = lax.rem(layer + o, freq_count)
            remote(
                stats_all.at[other], stats_all.at[other], gather_send.at[o], gather_sem.at[other], freq=other
            ).wait_recv()
        for slot in range(per_device):
            lag_rows, gradient = [
                stats_all[:, slot, i].reshape(freq_count * blocks, LANES) for i in range(2)
            ]
            found = solve(weight, lag_rows, gradient, matrix.at[slot])
            solved[...] = found.reshape(freq_count, blocks, LANES)
            taps[me * per_device + slot] = solved[layer]
        for o in range(1, trace_count):
            taps_copy(o).start()

    if owners == trace_count:
        solve_own()
    else:
        pl.when(owns)(solve_own)

    for o in range(1, trace_count):
        other = lax.rem(me + o, trace_count)

        def arrived():
            own = pl.ds(other * per_device, per_device)
            remote(taps.at[own], taps.at[own], taps_send.at[o], taps_sem.at[other], trace=other).wait_recv()

        if owners == trace_count:
            arrived()
        else:
            pl.when(other < owners)(arrived)
    taps_out[...] = taps[:shots]

    def drain(s, carry):
        for side in range(2):

            @pl.when(sends[side])
            def _():
                halo_copy(side, s).wait_send()

        owner = s // per_device
        for end, where in ((0, 0), (1, last)):

            @pl.when((me == where) & (owner != where))
            def _():
                corner_copy(end, s, owner, s % per_device).wait_send()

        @pl.when(me != owner)
        def _():
            stats_copy(s).wait_send()

        pltpu.make_async_copy(spec.at[s], spec_any.at[s], spec_sem.at[s]).wait()
        return carry

    lax.fori_loop(0, shots, drain, 0)

    def drain_own():
        for o in range(1, freq_count):
            relay_copy(o).wait_send()
            gather_copy(o).wait_send()
        for o in range(1, trace_count):
            taps_copy(o).wait_send()

    if owners == trace_count:
        drain_own()
    else:
        pl.when(owns)(drain_own)


def forward_kernel(taps_ref, wide, low, back, spec_ref, rec_ref, out_ref, filters_ref, shaped):
    shots, blocks, _ = taps_ref.shape
    s = pl.program_id(0)

    @pl.when(s == 0)
    def _():
        high, rest = split(taps_ref[...].reshape(shots * blocks, LANES))
        value = product(jnp.concatenate([high, rest], 1), wide[...]) + product(high, low[...])
        shaped[...] = value.reshape(shots, blocks, 4 * LANES)

    own = taps_ref[s]
    filters_ref[0, 0] = own[:, :TAPS]
    filters_ref[0, 1] = turn(own, TAPS)[:, :TAPS]
    for b in range(blocks):
        rows = slice(b * FB, (b + 1) * FB)
        w_ac, w_as, w_bc, w_bs = [spec_ref[0, i, rows, :] for i in range(4)]
        h_ac, h_as, h_bc, h_bs = [shaped[s, b : b + 1, i * LANES : (i + 1) * LANES] for i in range(4)]
        y_ac = h_ac * w_ac - h_as * w_as - h_bc * w_bc + h_bs * w_bs
        y_as = h_ac * w_as + h_as * w_ac - h_bc * w_bs - h_bs * w_bc
        y_bc = h_ac * w_bc - h_as * w_bs + h_bc * w_ac - h_bs * w_as
        y_bs = h_ac * w_bs + h_as * w_bc + h_bc * w_as + h_bs * w_ac
        both = jnp.concatenate(
            [jnp.concatenate([y_ac, y_as], 1), jnp.concatenate([y_bc, y_bs], 1)], 0
        )
        value = product(jnp.concatenate(split(both), 0), back[...])
        value = value[: 2 * FB] + value[2 * FB :]
        applied = value[:, :LANES] + value[:, LANES:]
        out_ref[0, 0, rows, :] = rec_ref[0, 0, rows, :] - applied[:FB]
        out_ref[0, 1, rows, :] = rec_ref[0, 1, rows, :] - applied[FB:]


def body(recorded, multiples):
    shots, parts, freq_rows, trace_rows = multiples.shape
    blocks = freq_rows // FB
    trace_count, freq_count = lax.axis_size("trace"), lax.axis_size("freq")
    weight = 0.5 * FB * trace_rows * trace_count
    per_device = -(-shots // trace_count)
    owners = -(-shots // per_device)
    pack_rows = freq_rows * HALF // LANES
    relay_at = min(2, shots - 1)

    tables = fit_tables()
    field = (shots, parts, freq_rows, trace_rows)
    dma = pltpu.SemaphoreType.DMA
    vmem = pl.BlockSpec(memory_space=pltpu.VMEM)
    anywhere = pl.BlockSpec(memory_space=pl.ANY)
    taps, spec = pl.pallas_call(
        functools.partial(fit_kernel, weight, trace_count, freq_count, per_device, relay_at),
        in_specs=[anywhere, anywhere] + [vmem] * len(tables),
        out_specs=[vmem, anywhere],
        out_shape=[
            jax.ShapeDtypeStruct((shots, blocks, LANES), F32),
            jax.ShapeDtypeStruct((shots, 4, freq_rows, LANES), F32),
        ],
        scratch_shapes=[
            pltpu.VMEM(field, F32),
            pltpu.VMEM(field, F32),
            pltpu.VMEM((2, shots, parts, pack_rows, LANES), F32),
            pltpu.VMEM((2, shots, parts, pack_rows, LANES), F32),
            pltpu.VMEM((shots, 4, freq_rows, LANES), F32),
            pltpu.VMEM((6, shots, blocks, LANES), F32),
            pltpu.VMEM((shots, HALF, blocks, LANES), F32),
            pltpu.VMEM((2, per_device, HALF, blocks, LANES), F32),
            pltpu.VMEM((freq_count, per_device, HALF, blocks, LANES), F32),
            pltpu.VMEM((shots, 2, blocks, LANES), F32),
            pltpu.VMEM((trace_count, per_device, 2, blocks, LANES), F32),
            pltpu.VMEM((freq_count, per_device, 2, blocks, LANES), F32),
            pltpu.VMEM((owners * per_device, blocks, LANES), F32),
            pltpu.VMEM((freq_count, blocks, LANES), F32),
            pltpu.VMEM((per_device, TAPS + 1, freq_count * blocks, LANES), F32),
            dma((shots,)),
            dma((shots,)),
            dma((shots,)),
            dma((2, shots)),
            dma((2, shots)),
            dma((shots,)),
            dma((2, per_device)),
            dma((freq_count,)),
            dma((freq_count,)),
            dma((shots,)),
            dma((trace_count, per_device)),
            dma((freq_count,)),
            dma((freq_count,)),
            dma((trace_count,)),
            dma((trace_count,)),
        ],
        compiler_params=pltpu.CompilerParams(
            collective_id=0, has_side_effects=True, vmem_limit_bytes=56 * 1024 * 1024
        ),
        name="fit",
    )(multiples, recorded, *[jnp.asarray(table) for table in tables])

    tables = forward_tables()
    block = pl.BlockSpec((1, parts, freq_rows, trace_rows), lambda s: (s, 0, 0, 0))
    fixed = [pl.BlockSpec(table.shape, lambda s: (0, 0)) for table in tables]
    return pl.pallas_call(
        forward_kernel,
        grid=(shots,),
        in_specs=[
            pl.BlockSpec((shots, blocks, LANES), lambda s: (0, 0, 0)),
            *fixed,
            pl.BlockSpec((1, 4, freq_rows, LANES), lambda s: (s, 0, 0, 0)),
            block,
        ],
        out_specs=[block, pl.BlockSpec((1, parts, blocks, TAPS), lambda s: (s, 0, 0, 0))],
        out_shape=[
            jax.ShapeDtypeStruct(field, F32),
            jax.ShapeDtypeStruct((shots, parts, blocks, TAPS), F32),
        ],
        scratch_shapes=[pltpu.VMEM((shots, blocks, 4 * LANES), F32)],
        name="forward",
    )(taps, *[jnp.asarray(table) for table in tables], spec, recorded)


def solution(mesh):
    spec = P(None, None, "freq", "trace")
    return jax.shard_map(
        body,
        mesh=mesh,
        in_specs=(spec, spec),
        out_specs=(spec, P(None, None, "freq", None)),
        check_vma=False,
    )
```

time: 152 us -> 60.7 us (0.40)
  starting transfers between devices: 28.2 us -> 0 us
  blocking collectives: 26.5 us -> 0 us
  waiting for transfers between devices: 18.7 us -> 0 us
  local copies, waits for them, and re-layouts: 7.28 us -> 0 us
  Pallas kernels: 67 us -> 59.8 us
  other arithmetic: 3.31 us -> 0 us
    all_gather x2 -> x0, blocking collectives: 26.5 us -> none  [the longest x1 17.3 us: body(): stats = lax.all_gather(stats, 'freq', axis=0)]
    all_to_all x1 -> x0, starting transfers between devices: 23.8 us -> none  [body(): lax.all_to_all(stats, 'trace', split_axis=0, concat_axis=0, tiled=True)]
    all_to_all x1 -> x0, waiting for transfers between devices: 16.8 us -> none  [body(): lax.all_to_all(stats, 'trace', split_axis=0, concat_axis=0, tiled=True)]
    pallas_call x3 -> x2, Pallas kernels: 67 us -> 59.8 us  [the longest x1 49.2 us: body(): pl.pallas_call(functools.partial(fit_kernel, weight, trace_count, freq_co...]
    split x1 -> x0, local copies, waits for them, and re-layouts: 4.97 us -> none  [packed(): return jnp.concatenate(jnp.split(value, count, axis=2), axis=3)]
    ppermute x2 -> x0, starting transfers between devices: 4.38 us -> none  [the longest x1 3.08 us: body(): left = lax.ppermute(packed(multiples[..., trace_rows - HALF:]), 'trace', up)]
    concatenate x2 -> x0, other arithmetic: 2.73 us -> none  [packed(): return jnp.concatenate(jnp.split(value, count, axis=2), axis=3)]
    ppermute x2 -> x0, waiting for transfers between devices: 1.88 us -> none  [the longest x1 1.88 us: body(): left = lax.ppermute(packed(multiples[..., trace_rows - HALF:]), 'trace', up)]
  transfers between devices with their start and end apart: 3 -> 0, of which waited for: 2 -> 0; matrix products, arithmetic and copies ran while one was open for 2% -> 0% of each run, Pallas kernels for 0% -> 0%
where the time goes in v1:
time: 60.7 us; the launch traced here: 60.5 us
  Pallas kernels  59.8 us (99%)
  between operations  0.64 us (1%)
    pallas_call x1, Pallas kernels, body(): pl.pallas_call(functools.partial(fit_kernel, weight, trace_count, freq_co...  49.2 us
    pallas_call x1, Pallas kernels, body(): pl.pallas_call(forward_kernel, grid=(shots,), in_specs=[pl.BlockSpec((sho...  10.6 us

profile of v1, /device:TPU:0, one launch (start us, length us, event | category | flops | bytes accessed | tf_op | source)
XLA Modules:
  0.0 60.5 jit_solution(5011324178829154660)
XLA Ops:
  0.6 49.2 %fit.1 = (f32[8,8,128]{2,1,0:T(8,128)}, f32[8,4,512,128]{3,2,1,0:T(8,128)}) custom-call(f32[8,2,512,128]{3,2,1,0:T(8,128)} %m_any.1, f32[8,2,512,128]{3,2,1,0:T(8,128)} %rec_ref.1, bf16[256,256]{1,0:T(8,128)(2,1)} %constant.16.clone.wide, bf16[128,256]{1,0:T(8,128)(2,1)} %constant.17.clone.low, bf16[256,256]{1,0:T(8,128)(2,1)} %constant.18.clone.tail, ...), custom_call_target="tpu_custom_call" | custom-call | tf_op jit(solution)/shard_map/fit/pallas_call | solution.py:625
  49.9 10.6 %forward.1 = (f32[8,2,512,128]{3,2,1,0:T(8,128)}, f32[8,2,8,64]{3,2,1,0:T(8,128)}) custom-call(f32[8,8,128]{2,1,0:T(8,128)} %get-tuple-element.4.taps_ref, bf16[256,512]{1,0:T(8,128)(2,1)} %constant.21.clone.wide, bf16[128,512]{1,0:T(8,128)(2,1)} %constant.22.clone.low, bf16[256,256]{1,0:T(8,128)(2,1)} %constant.23.clone.back, ...), custom_call_target="tpu_custom_call" | custom-call | tf_op jit(solution)/shard_map/forward/pallas_call | solution.py:674

commit v2 on v1

v2 whole, which is shorter than its diff:
```python
import functools

import jax
import jax.numpy as jnp
import numpy as np
from jax import lax
from jax.experimental import pallas as pl
from jax.experimental.pallas import tpu as pltpu
from jax.sharding import PartitionSpec as P

FB = 64
TAPS = 64
ITERS = 3
HALF = TAPS // 2
LANES = 128
POINTS = 2 * LANES
F32 = jnp.float32
BF16 = jnp.bfloat16
MESH = pl.DeviceIdType.MESH


def lanes_of(shape):
    return lax.broadcasted_iota(jnp.int32, shape, len(shape) - 1)


def turn(value, shift):
    shift = shift % LANES
    return value if shift == 0 else pltpu.roll(value, shift, 1)


def split(value):
    high = value.astype(BF16)
    return high, (value - high.astype(F32)).astype(BF16)


def waves(positions):
    phase = (2 * np.pi / POINTS) * np.outer(np.asarray(positions), np.arange(LANES) + 0.5)
    return np.cos(phase), np.sin(phase)


def both_waves(positions):
    return np.concatenate(waves(positions), 1)


def halves(table):
    high = table.astype(np.float32).astype(BF16)
    return high, (table - high.astype(np.float64)).astype(np.float32).astype(BF16)


def all_tables():
    high, low = halves(both_waves(np.arange(LANES)))
    tail_high, tail_low = halves(both_waves(LANES + np.arange(TAPS)))
    lag = np.where(np.arange(LANES) < TAPS, np.arange(LANES), LANES - np.arange(LANES))
    used = (np.arange(LANES) != TAPS) / LANES
    sign = np.where(np.arange(LANES) < TAPS, -2.0, 2.0)
    lag_cos, lag_sin = waves(lag)
    right = both_waves(-1 - np.arange(TAPS)).T / LANES
    none = np.zeros_like(right)
    shape_high, shape_low = halves(both_waves(np.arange(TAPS)))
    parts = dict(
        wide=[high, high],
        low=[low],
        tail=[tail_high, tail_high, tail_low, np.zeros_like(tail_low)],
        power=[np.concatenate(halves(lag_cos.T * used), 1)],
        cross=[np.concatenate(halves(lag_sin.T * (sign * used)), 1)],
        sides=[np.concatenate(halves(np.block([[right, none], [none, right]])), 1)],
        shape=[shape_high, shape_high, shape_low, np.zeros_like(shape_low)],
        back=[np.concatenate(halves(both_waves(TAPS + np.arange(LANES)).T / LANES), 1)],
    )
    parts = {name: np.concatenate(part, 0) for name, part in parts.items()}
    runs, start = {}, 0
    for name, part in parts.items():
        runs[name] = slice(start, start + part.shape[0])
        start += part.shape[0]
    return np.concatenate(list(parts.values()), 0), runs


def over_first(left, right):
    return lax.dot_general(left, right, (((0,), (0,)), ((), ())), preferred_element_type=F32)


def product(left, right):
    return jnp.dot(left, right, preferred_element_type=F32)


def exact(left, right):
    return jnp.dot(left, right, precision=lax.Precision.HIGHEST, preferred_element_type=F32)


def mirror(total):
    rows = lax.broadcasted_iota(jnp.int32, (LANES, LANES), 0)
    return (rows + lanes_of((LANES, LANES)) == total).astype(F32)


def total_of(value):
    return jnp.sum(jnp.sum(value, axis=1, keepdims=True), axis=0, keepdims=True)


def column_sum(value):
    return jnp.sum(value, axis=0, keepdims=True)


def pack_edges(m, edge, s):
    freq_rows = m.shape[2]
    groups = LANES // HALF
    rows = freq_rows // groups
    lane = lanes_of((rows, LANES))
    for part in range(2):
        for side in range(2):
            packed = None
            for g in range(groups):
                shift = HALF * g + HALF if side == 0 else HALF * g
                value = turn(m[s, part, g * rows : (g + 1) * rows, :], shift)
                packed = value if packed is None else jnp.where(lane >= HALF * g, value, packed)
            edge[side, s, part] = packed


def corners(m, ends, corner, s, at_last):
    freq_rows = m.shape[2]
    wide = (freq_rows, LANES)
    lane = lanes_of(wide)
    real = pltpu.roll(m[s, 0], jnp.where(at_last, HALF, 0), 1)
    imag = pltpu.roll(m[s, 1], jnp.where(at_last, 2 * HALF, HALF), 1)
    both = jnp.where(lane < HALF, real, imag)
    rest = both - both.astype(BF16).astype(F32)
    ends[...] = jnp.where(lane < TAPS, both, turn(rest, TAPS)).astype(BF16)
    lane = lanes_of((HALF, LANES))
    for b in range(freq_rows // FB):
        part = ends[b * FB : (b + 1) * FB, :]
        gram = over_first(part, part)
        gram = gram[:TAPS] + gram[TAPS:]
        gram = gram + turn(gram, TAPS)
        one, two = gram[:HALF], turn(gram[HALF:], HALF)
        value = jnp.where(lane % TAPS < HALF, one + two, one - two)
        corner[s, :, b, :] = jnp.where(
            lane[: HALF // 2] < TAPS, value[: HALF // 2], value[HALF // 2 :]
        )


def joined_corners(left, right):
    shape = left.shape
    lane = lanes_of(shape)

    def moved(value, shift):
        return pltpu.roll(value, shift % LANES, 2)

    def pick(*values):
        result = values[0]
        for i in range(1, 4):
            result = jnp.where(lane >= i * HALF, values[i], result)
        return result

    first = pick(right, moved(left, HALF), moved(right, HALF), moved(left, TAPS))
    second = pick(moved(right, TAPS), moved(left, -HALF), moved(right, -HALF), left)
    value = jnp.concatenate([first, second], 0)
    place = lanes_of(value.shape) % TAPS
    step = 1
    while step < HALF:
        none = jnp.zeros((step,) + shape[1:], F32)
        later = jnp.concatenate([moved(value[step:], -step), none], 0)
        sooner = jnp.concatenate([none, moved(value[:-step], step)], 0)
        value = value + jnp.where(
            place < HALF - step, later, jnp.where(place >= HALF + step, sooner, 0.0)
        )
        step *= 2
    return value


def fourfold(value, table):
    count = value.shape[0]
    both = product(jnp.concatenate(split(value), 0), table)
    both = both[:count] + both[count:]
    return both[:, :LANES] + both[:, LANES:]


def threefold(value, table):
    top = value.astype(BF16)
    rest = turn(value - top.astype(F32), TAPS)
    mixed = jnp.where(lanes_of(value.shape) < TAPS, value, rest).astype(BF16)
    return product(jnp.concatenate([mixed, top], 1), table)


def statistics(m, rec, halo, spec, sums, table, s):
    freq_rows = m.shape[2]
    group_rows = freq_rows * HALF // LANES
    lane = lanes_of((FB, LANES))
    for b in range(freq_rows // FB):
        rows = slice(b * FB, (b + 1) * FB)
        group, first = (b * FB) // group_rows, (b * FB) % group_rows
        near = slice(first, first + FB)
        starts, tails = [], []
        for part in range(2):
            turned = turn(m[s, part, rows, :], HALF)
            left = turn(halo[0, s, part, near, :], -HALF * group)
            right = turn(halo[1, s, part, near, :], HALF - HALF * group)
            starts.append(jnp.where(lane < HALF, left, turned))
            tails.append(jnp.where(lane < HALF, turned, right))
        high, rest = split(jnp.concatenate(starts + [rec[s, 0, rows, :], rec[s, 1, rows, :]], 0))
        main = product(jnp.concatenate([high, rest], 1), table("wide")) + product(high, table("low"))
        last = threefold(jnp.concatenate(tails, 0), table("tail"))

        def parts(value, first):
            return value[first : first + FB, :LANES], value[first : first + FB, LANES:]

        s_all = parts(main, 0) + parts(main, FB)
        t_all = parts(last, 0) + parts(last, FB)
        r_ac, r_as, r_bc, r_bs = parts(main, 2 * FB) + parts(main, 3 * FB)
        w_all = [x + y for x, y in zip(s_all, t_all)]
        for i in range(4):
            spec[s, i, rows, :] = w_all[i]
        w_ac, w_as, w_bc, w_bs = w_all
        t_ac, t_as, t_bc, t_bs = t_all
        power = sum(x * (w + t) for x, w, t in zip(s_all, w_all, t_all))
        cross = (w_ac * w_bs - w_as * w_bc) - (t_ac * t_bs - t_as * t_bc)
        found = [
            power,
            cross,
            w_ac * r_ac + w_as * r_as + w_bc * r_bc + w_bs * r_bs,
            w_ac * r_as - w_as * r_ac + w_bc * r_bs - w_bs * r_bc,
            w_ac * r_bc + w_as * r_bs - w_bc * r_ac - w_bs * r_as,
            w_ac * r_bs - w_as * r_bc - w_bc * r_as + w_bs * r_ac,
        ]
        for i in range(6):
            sums[i, b : b + 1, :] = column_sum(found[i])


def prepare_corners(corner, matrix):
    blocks = corner.shape[0] * corner.shape[2]

    def row(r):
        return corner[:, r, :, :].reshape(blocks, LANES)

    lane = lanes_of((blocks, LANES))
    place = lane % TAPS
    is_real = lane < TAPS
    for i in range(HALF):
        value = row(i)
        if i:
            moved = jnp.where(place < HALF - 1, turn(value, -1), 0.0)
            matrix[i - 1] = jnp.where(is_real, -moved, moved)
        value = jnp.where(place < HALF, 0.0, value)
        matrix[HALF + i] = jnp.where(is_real, -value, value)
    matrix[HALF - 1] = jnp.zeros((blocks, LANES), F32)
    right = jnp.where(place < HALF, row(0), 0.0)
    add_real = jnp.where(lane < HALF, right, 0.0)
    add_imag = jnp.where(lane < HALF, turn(right, TAPS), 0.0)
    back = mirror(LANES)
    matrix[TAPS] = jnp.where(is_real, add_real, exact(add_real, back))
    matrix[TAPS + 1] = jnp.where(is_real, -add_imag, exact(add_imag, back))


def solve(weight, toep_real, toep_imag, gradient, matrix):
    blocks = gradient.shape[0]
    lane = lanes_of((blocks, LANES))
    is_real = lane < TAPS
    toep_real = toep_real + matrix[TAPS]
    toep_imag = toep_imag + matrix[TAPS + 1]
    for t in range(TAPS):
        matrix[t] += jnp.where(is_real, turn(toep_real, t), turn(toep_imag, TAPS + t))

    filters = jnp.zeros((blocks, LANES), F32)
    direction = norm_now = None
    none = jnp.zeros((1, LANES), F32)
    for iteration in range(ITERS):
        norm_next = total_of(gradient * gradient)
        if iteration == 0:
            direction = gradient
        else:
            direction = gradient + (norm_next / norm_now) * direction
        norm_now = norm_next
        by_real = jnp.zeros((blocks, LANES), F32)
        by_imag = jnp.zeros((blocks, LANES), F32)
        for t in range(TAPS):
            by_real = by_real + direction[:, t : t + 1] * matrix[t]
            by_imag = by_imag + direction[:, TAPS + t : TAPS + t + 1] * matrix[t]
        by_imag = turn(by_imag, TAPS)
        normal = by_real + jnp.where(is_real, -by_imag, by_imag)
        before = jnp.concatenate([none, direction[:-1]], 0)
        after = jnp.concatenate([direction[1:], none], 0)
        normal = normal + weight * (2.0 * direction - before - after)
        step_len = norm_now / total_of(direction * normal)
        filters = filters + step_len * direction
        gradient = gradient - step_len * normal
    rows = lax.broadcasted_iota(jnp.int32, (LANES, LANES), 0)
    columns = lanes_of((LANES, LANES))
    flip = (rows + columns == jnp.where(columns < TAPS, TAPS - 1, 3 * TAPS - 1)).astype(F32)
    return exact(filters, flip)


def shaped_back(taps_row, rec, spec, table, s):
    blocks = taps_row.shape[0]
    shape = threefold(jnp.concatenate([taps_row, turn(taps_row, TAPS)], 0), table("shape"))
    shape = jnp.concatenate([shape[:blocks], shape[blocks:]], 1)
    for b in range(rec.shape[2] // FB):
        rows = slice(b * FB, (b + 1) * FB)
        w_ac, w_as, w_bc, w_bs = [spec[s, i, rows, :] for i in range(4)]
        h_ac, h_as, h_bc, h_bs = [shape[b : b + 1, i * LANES : (i + 1) * LANES] for i in range(4)]
        y_ac = h_ac * w_ac - h_as * w_as - h_bc * w_bc + h_bs * w_bs
        y_as = h_ac * w_as + h_as * w_ac - h_bc * w_bs - h_bs * w_bc
        y_bc = h_ac * w_bc - h_as * w_bs + h_bc * w_ac - h_bs * w_as
        y_bs = h_ac * w_bs + h_as * w_bc + h_bc * w_as + h_bs * w_ac
        both = jnp.concatenate(
            [jnp.concatenate([y_ac, y_as], 1), jnp.concatenate([y_bc, y_bs], 1)], 0
        )
        applied = fourfold(both, table("back"))
        rec[s, 0, rows, :] = rec[s, 0, rows, :] - applied[:FB]
        rec[s, 1, rows, :] = rec[s, 1, rows, :] - applied[FB:]


def fit_kernel(
    weight,
    trace_count,
    freq_count,
    runs,
    m_any,
    rec_any,
    table_any,
    out_any,
    filters_out,
    m,
    rec,
    edge,
    halo,
    spec,
    sums,
    corner,
    corner_in,
    corner_all,
    stats,
    stats_in,
    stats_all,
    taps,
    solved,
    matrix,
    tables,
    ends_v,
    table_sem,
    m_sem,
    rec_sem,
    out_sem,
    edge_send,
    halo_sem,
    corner_send,
    corner_sem,
    relay_send,
    relay_sem,
    stats_send,
    stats_sem,
    gather_send,
    gather_sem,
    taps_send,
    taps_sem,
):
    shots = m.shape[0]
    blocks = m.shape[2] // FB
    last = trace_count - 1
    me = lax.axis_index("trace")
    layer = lax.axis_index("freq")
    owns = me < shots
    ends = ((0, 0), (1, last))

    def remote(source, target, send, arrive, **where):
        return pltpu.make_async_remote_copy(
            src_ref=source,
            dst_ref=target,
            send_sem=send,
            recv_sem=arrive,
            device_id=where,
            device_id_type=MESH,
        )

    def local(source, target, sem, s):
        return pltpu.make_async_copy(source.at[s], target.at[s], sem.at[s])

    for s in range(shots):
        local(m_any, m, m_sem, s).start()
    table_copy = pltpu.make_async_copy(table_any, tables, table_sem)
    table_copy.start()
    for s in range(shots):
        local(rec_any, rec, rec_sem, s).start()

    def table(name):
        return tables[runs[name], :]

    barrier = pltpu.get_barrier_semaphore()
    for o in range(1, trace_count):
        pl.semaphore_signal(
            barrier, inc=1, device_id={"trace": lax.rem(me + o, trace_count)}, device_id_type=MESH
        )
    for o in range(1, freq_count):
        pl.semaphore_signal(
            barrier, inc=1, device_id={"freq": lax.rem(layer + o, freq_count)}, device_id_type=MESH
        )

    @pl.when(me == 0)
    def _():
        halo[0] = jnp.zeros(halo.shape[1:], F32)

    @pl.when(me == last)
    def _():
        halo[1] = jnp.zeros(halo.shape[1:], F32)

    pl.semaphore_wait(barrier, trace_count + freq_count - 2)

    def halo_copy(side, s):
        other = jnp.minimum(me + 1, last) if side == 0 else jnp.maximum(me - 1, 0)
        return remote(
            edge.at[side, s], halo.at[side, s], edge_send.at[side, s], halo_sem.at[side, s], trace=other
        )

    def corner_copy(end, s, owner):
        return remote(corner.at[s], corner_in.at[end], corner_send.at[s], corner_sem.at[end], trace=owner)

    def relay_copy(o):
        return remote(
            corner_all.at[layer],
            corner_all.at[layer],
            relay_send.at[o],
            relay_sem.at[layer],
            freq=lax.rem(layer + o, freq_count),
        )

    def stats_copy(s):
        return remote(stats.at[s], stats_in.at[me], stats_send.at[s], stats_sem.at[me], trace=s)

    def gather_copy(o):
        return remote(
            stats_all.at[layer],
            stats_all.at[layer],
            gather_send.at[o],
            gather_sem.at[layer],
            freq=lax.rem(layer + o, freq_count),
        )

    def taps_copy(o):
        return remote(
            taps.at[me], taps.at[me], taps_send.at[o], taps_sem.at[me], trace=lax.rem(me + o, trace_count)
        )

    sends = (me < last, me > 0)
    receives = (me > 0, me < last)

    def start_halo(s):
        for side in range(2):

            @pl.when(sends[side])
            def _():
                halo_copy(side, s).start()

    def send_edges(s, carry):
        local(m_any, m, m_sem, s).wait()

        @pl.when((me == 0) | (me == last))
        def _():
            corners(m, ends_v, corner, s, me == last)
            for end, where in ends:

                @pl.when((me == where) & (s != where))
                def _():
                    corner_copy(end, s, s).start()

                @pl.when((me == where) & (s == where))
                def _():
                    corner_in[end] = corner[s]

        pack_edges(m, edge, s)
        start_halo(s)
        return carry

    lax.fori_loop(0, shots, send_edges, 0)

    def measure(s):
        local(rec_any, rec, rec_sem, s).wait()
        for side in range(2):

            @pl.when(receives[side])
            def _():
                halo_copy(side, s).wait_recv()

        statistics(m, rec, halo, spec, sums, table, s)
        stats[s, 0] = fourfold(sums[0], table("power"))
        stats[s, 1] = fourfold(sums[1], table("cross"))
        stats[s, 2] = fourfold(jnp.concatenate([sums[i] for i in range(2, 6)], 1), table("sides"))

        @pl.when(me != s)
        def _():
            stats_copy(s).start()

    def relay():
        for end, where in ends:

            @pl.when(me != where)
            def _():
                corner_copy(end, 0, me).wait_recv()

        corner_all[layer] = joined_corners(corner_in[0], corner_in[1])
        for o in range(1, freq_count):
            relay_copy(o).start()

    def prepare():
        for o in range(1, freq_count):
            other = lax.rem(layer + o, freq_count)
            remote(
                corner_all.at[other], corner_all.at[other], relay_send.at[o], relay_sem.at[other], freq=other
            ).wait_recv()
        prepare_corners(corner_all, matrix)

    def gather():
        whole = stats[me]
        for o in range(1, trace_count):
            other = lax.rem(me + o, trace_count)
            remote(
                stats.at[0], stats_in.at[other], stats_send.at[0], stats_sem.at[other], trace=other
            ).wait_recv()
            whole = whole + stats_in[other]
        stats_all[layer] = whole
        for o in range(1, freq_count):
            gather_copy(o).start()

    def solve_own():
        for o in range(1, freq_count):
            other = lax.rem(layer + o, freq_count)
            remote(
                stats_all.at[other], stats_all.at[other], gather_send.at[o], gather_sem.at[other], freq=other
            ).wait_recv()
        rows = [stats_all[:, i].reshape(freq_count * blocks, LANES) for i in range(3)]
        solved[...] = solve(weight, *rows, matrix).reshape(freq_count, blocks, LANES)
        taps[me] = solved[layer]
        for o in range(1, trace_count):
            taps_copy(o).start()

    def finish(s):
        @pl.when(me != s)
        def _():
            remote(taps.at[s], taps.at[s], taps_send.at[0], taps_sem.at[s], trace=s).wait_recv()

        own = taps[s]
        filters_out[s, 0] = own[:, :TAPS]
        filters_out[s, 1] = turn(own, TAPS)[:, :TAPS]
        shaped_back(own, rec, spec, table, s)
        local(rec, out_any, out_sem, s).start()

    relay_at = jnp.minimum(me, 1)

    def measure_step(s, carry):
        measure(s)
        pl.when(owns & (s == relay_at))(relay)
        return carry

    def finish_step(s, carry):
        finish(s)
        return carry

    table_copy.wait()
    lax.fori_loop(0, shots, measure_step, 0)

    @pl.when(owns)
    def _():
        gather()
        prepare()
        solve_own()

    lax.fori_loop(0, shots, finish_step, 0)

    def drain(s, carry):
        for side in range(2):

            @pl.when(sends[side])
            def _():
                halo_copy(side, s).wait_send()

        for end, where in ends:

            @pl.when((me == where) & (s != where))
            def _():
                corner_copy(end, s, s).wait_send()

        @pl.when(me != s)
        def _():
            stats_copy(s).wait_send()

        local(rec, out_any, out_sem, s).wait()
        return carry

    lax.fori_loop(0, shots, drain, 0)

    @pl.when(owns)
    def _():
        for o in range(1, freq_count):
            relay_copy(o).wait_send()
            gather_copy(o).wait_send()
        for o in range(1, trace_count):
            taps_copy(o).wait_send()


def body(recorded, multiples):
    shots, parts, freq_rows, trace_rows = multiples.shape
    blocks = freq_rows // FB
    trace_count, freq_count = lax.axis_size("trace"), lax.axis_size("freq")
    assert shots <= trace_count
    weight = 0.5 * FB * trace_rows * trace_count
    pack_rows = freq_rows * HALF // LANES

    table, runs = all_tables()
    field = (shots, parts, freq_rows, trace_rows)
    dma = pltpu.SemaphoreType.DMA
    vmem = pl.BlockSpec(memory_space=pltpu.VMEM)
    anywhere = pl.BlockSpec(memory_space=pl.ANY)
    return pl.pallas_call(
        functools.partial(fit_kernel, weight, trace_count, freq_count, runs),
        in_specs=[anywhere, anywhere, anywhere],
        out_specs=[anywhere, vmem],
        out_shape=[
            jax.ShapeDtypeStruct(field, F32),
            jax.ShapeDtypeStruct((shots, parts, blocks, TAPS), F32),
        ],
        scratch_shapes=[
            pltpu.VMEM(field, F32),
            pltpu.VMEM(field, F32),
            pltpu.VMEM((2, shots, parts, pack_rows, LANES), F32),
            pltpu.VMEM((2, shots, parts, pack_rows, LANES), F32),
            pltpu.VMEM((shots, 4, freq_rows, LANES), F32),
            pltpu.VMEM((6, blocks, LANES), F32),
            pltpu.VMEM((shots, HALF // 2, blocks, LANES), F32),
            pltpu.VMEM((2, HALF // 2, blocks, LANES), F32),
            pltpu.VMEM((freq_count, HALF, blocks, LANES), F32),
            pltpu.VMEM((shots, 3, blocks, LANES), F32),
            pltpu.VMEM((trace_count, 3, blocks, LANES), F32),
            pltpu.VMEM((freq_count, 3, blocks, LANES), F32),
            pltpu.VMEM((shots, blocks, LANES), F32),
            pltpu.VMEM((freq_count, blocks, LANES), F32),
            pltpu.VMEM((TAPS + 2, freq_count * blocks, LANES), F32),
            pltpu.VMEM(table.shape, BF16),
            pltpu.VMEM((freq_rows, LANES), BF16),
            dma,
            dma((shots,)),
            dma((shots,)),
            dma((shots,)),
            dma((2, shots)),
            dma((2, shots)),
            dma((shots,)),
            dma((2,)),
            dma((freq_count,)),
            dma((freq_count,)),
            dma((shots,)),
            dma((trace_count,)),
            dma((freq_count,)),
            dma((freq_count,)),
            dma((trace_count,)),
            dma((shots,)),
        ],
        compiler_params=pltpu.CompilerParams(
            collective_id=0, has_side_effects=True, vmem_limit_bytes=48000000
        ),
        name="fit",
    )(multiples, recorded, jnp.asarray(table))


def solution(mesh):
    spec = P(None, None, "freq", "trace")
    return jax.shard_map(
        body,
        mesh=mesh,
        in_specs=(spec, spec),
        out_specs=(spec, P(None, None, "freq", None)),
        check_vma=False,
    )
```

time: 60.7 us -> 52.6 us (0.87)
  Pallas kernels: 59.8 us -> 48 us
  local copies, waits for them, and re-layouts: 0 us -> 3.84 us
    pallas_call x1 -> x0, Pallas kernels: 10.6 us -> none  [body(): pl.pallas_call(forward_kernel, grid=(shots,), in_specs=[pl.BlockSpec((sho...]
    unnamed x0 -> x4, local copies, waits for them, and re-layouts: none -> 3.84 us
    pallas_call x1, Pallas kernels: 49.2 us -> 48 us  [body(): pl.pallas_call(functools.partial(fit_kernel, weight, trace_count, freq_co...]
where the time goes in v2:
time: 52.6 us; the launch traced here: 52.5 us
  Pallas kernels  48 us (91%)
  local copies, waits for them, and re-layouts  3.84 us (7%)
  between operations  0.65 us (1%)
    pallas_call x1, Pallas kernels, body(): pl.pallas_call(functools.partial(fit_kernel, weight, trace_count, freq_co...  48 us
    unnamed x4, local copies, waits for them, and re-layouts  3.84 us

profile of v2, /device:TPU:0, one launch (start us, length us, event | category | flops | bytes accessed | tf_op | source)
XLA Modules:
  0.0 52.5 jit_solution(11146524827759195829)
XLA Ops:
  0.6 0.0 copy-start
  0.6 1.2 %copy-done = bf16[1920,256]{1,0:T(8,128)(2,1)S(1)} copy-done((bf16[1920,256]{1,0:T(8,128)(2,1)S(1)}, bf16[1920,256]{1,0:T(8,128)(2,1)}, u32[]{:S(2)}) %copy-start) | copy-done | bytes 983064
  1.8 48.0 %fit.1 = (f32[8,2,512,128]{3,2,1,0:T(8,128)S(1)}, f32[8,2,8,64]{3,2,1,0:T(8,128)S(1)}) custom-call(f32[8,2,512,128]{3,2,1,0:T(8,128)} %m_any.1, f32[8,2,512,128]{3,2,1,0:T(8,128)} %rec_any.1, bf16[1920,256]{1,0:T(8,128)(2,1)S(1)} %copy-done), custom_call_target="tpu_custom_call" | custom-call | tf_op jit(solution)/shard_map/fit/pallas_call | solution.py:609
  49.8 2.0 %copy.7 = f32[8,2,512,128]{3,2,1,0:T(8,128)} copy(f32[8,2,512,128]{3,2,1,0:T(8,128)S(1)} %get-tuple-element.4) | data formatting | bytes 8388608
  51.8 0.6 %copy.8 = f32[8,2,8,64]{3,2,1,0:T(8,128)} copy(f32[8,2,8,64]{3,2,1,0:T(8,128)S(1)} %get-tuple-element.5) | data formatting | bytes 65536
Async XLA Ops:
  0.6 1.2 %copy-start = (bf16[1920,256]{1,0:T(8,128)(2,1)S(1)}, bf16[1920,256]{1,0:T(8,128)(2,1)}, u32[]{:S(2)}) copy-start(bf16[1920,256]{1,0:T(8,128)(2,1)} %constant.2.clone.table_any) | copy-start | bytes 2949124

commit v3 on v2

--- a/solution.py
+++ b/solution.py
@@ -287,10 +287,15 @@
     return exact(filters, flip)
 
 
-def shaped_back(taps_row, rec, spec, table, s):
-    blocks = taps_row.shape[0]
-    shape = threefold(jnp.concatenate([taps_row, turn(taps_row, TAPS)], 0), table("shape"))
-    shape = jnp.concatenate([shape[:blocks], shape[blocks:]], 1)
+def shapes(taps, table):
+    shots, blocks, _ = taps.shape
+    rows = taps.reshape(shots * blocks, LANES)
+    value = threefold(jnp.concatenate([rows, turn(rows, TAPS)], 0), table("shape"))
+    value = jnp.concatenate([value[: shots * blocks], value[shots * blocks :]], 1)
+    return value.reshape(shots, blocks, 2 * POINTS)
+
+
+def shaped_back(shape, rec, spec, table, s):
     for b in range(rec.shape[2] // FB):
         rows = slice(b * FB, (b + 1) * FB)
         w_ac, w_as, w_bc, w_bs = [spec[s, i, rows, :] for i in range(4)]
@@ -305,6 +310,10 @@
         applied = fourfold(both, table("back"))
         rec[s, 0, rows, :] = rec[s, 0, rows, :] - applied[:FB]
         rec[s, 1, rows, :] = rec[s, 1, rows, :] - applied[FB:]
+
+
+def detour_count(shots, trace_count):
+    return (shots - 1) // 2 if trace_count >= 4 else 0
 
 
 def fit_kernel(
@@ -334,6 +343,9 @@
     matrix,
     tables,
     ends_v,
+    passing,
+    pass_send,
+    pass_sem,
     table_sem,
     m_sem,
     rec_sem,
@@ -440,18 +452,59 @@
     sends = (me < last, me > 0)
     receives = (me > 0, me < last)
 
+    middle = trace_count // 2
+    detours = detour_count(shots, trace_count)
+
+    def detoured(side, s):
+        if not detours:
+            return False
+        return (me == (middle - 1 if side == 0 else middle)) & (s > 0) & (lax.rem(s, 2) == 0)
+
+    def detour_copy(side, s):
+        i = jnp.maximum(s // 2 - 1, 0)
+        return remote(
+            edge.at[side, s],
+            passing.at[i],
+            edge_send.at[side, s],
+            pass_sem.at[i],
+            trace=last if side == 0 else 0,
+        )
+
+    def pass_copy(side, i):
+        s = 2 * i + 2
+        return remote(
+            passing.at[i],
+            halo.at[side, s],
+            pass_send.at[i],
+            halo_sem.at[side, s],
+            trace=middle if side == 0 else middle - 1,
+        )
+
+    passes = (me == last, me == 0)
+
     def start_halo(s):
         for side in range(2):
 
-            @pl.when(sends[side])
+            @pl.when(sends[side] & jnp.logical_not(detoured(side, s)))
             def _():
                 halo_copy(side, s).start()
 
-    def send_edges(s, carry):
-        local(m_any, m, m_sem, s).wait()
-
-        @pl.when((me == 0) | (me == last))
-        def _():
+            @pl.when(detoured(side, s))
+            def _():
+                detour_copy(side, s).start()
+
+    def pass_on(i):
+        for side in range(2):
+
+            @pl.when(passes[side])
+            def _():
+                detour_copy(side, 2 * i + 2).wait_recv()
+                pass_copy(side, i).start()
+
+    @pl.when((me == 0) | (me == last))
+    def _():
+        def send_corners(s, carry):
+            local(m_any, m, m_sem, s).wait()
             corners(m, ends_v, corner, s, me == last)
             for end, where in ends:
 
@@ -463,11 +516,22 @@
                 def _():
                     corner_in[end] = corner[s]
 
+            return carry
+
+        lax.fori_loop(0, shots, send_corners, 0)
+
+    def send_edges(s, carry):
+        @pl.when((me > 0) & (me < last))
+        def _():
+            local(m_any, m, m_sem, s).wait()
+
         pack_edges(m, edge, s)
         start_halo(s)
         return carry
 
     lax.fori_loop(0, shots, send_edges, 0)
+    for i in range(detours):
+        pass_on(i)
 
     def measure(s):
         local(rec_any, rec, rec_sem, s).wait()
@@ -529,7 +593,7 @@
         for o in range(1, trace_count):
             taps_copy(o).start()
 
-    def finish(s):
+    def take_taps(s):
         @pl.when(me != s)
         def _():
             remote(taps.at[s], taps.at[s], taps_send.at[0], taps_sem.at[s], trace=s).wait_recv()
@@ -537,18 +601,25 @@
         own = taps[s]
         filters_out[s, 0] = own[:, :TAPS]
         filters_out[s, 1] = turn(own, TAPS)[:, :TAPS]
-        shaped_back(own, rec, spec, table, s)
-        local(rec, out_any, out_sem, s).start()
-
-    relay_at = jnp.minimum(me, 1)
+
+    at_once = 2 if shots % 2 == 0 else 1
+
+    def finish(i, carry):
+        group = [i * at_once + s for s in range(at_once)]
+        for s in group:
+            take_taps(s)
+        shaped = shapes(taps[pl.ds(i * at_once, at_once)], table)
+        for s in range(at_once):
+            shaped_back(shaped[s], rec, spec, table, group[s])
+        for s in group:
+            local(rec, out_any, out_sem, s).start()
+        return carry
+
+    relay_at = jnp.minimum(me, 2)
 
     def measure_step(s, carry):
         measure(s)
         pl.when(owns & (s == relay_at))(relay)
-        return carry
-
-    def finish_step(s, carry):
-        finish(s)
         return carry
 
     table_copy.wait()
@@ -560,14 +631,22 @@
         prepare()
         solve_own()
 
-    lax.fori_loop(0, shots, finish_step, 0)
+    lax.fori_loop(0, shots // at_once, finish, 0)
 
     def drain(s, carry):
         for side in range(2):
 
-            @pl.when(sends[side])
+            @pl.when(sends[side] & jnp.logical_not(detoured(side, s)))
             def _():
                 halo_copy(side, s).wait_send()
+
+            @pl.when(detoured(side, s))
+            def _():
+                detour_copy(side, s).wait_send()
+
+            @pl.when(passes[side] & (s < detours))
+            def _():
+                pass_copy(side, jnp.minimum(s, detours - 1)).wait_send()
 
         for end, where in ends:
 
@@ -600,6 +679,7 @@
     assert shots <= trace_count
     weight = 0.5 * FB * trace_rows * trace_count
     pack_rows = freq_rows * HALF // LANES
+    detours = detour_count(shots, trace_count)
 
     table, runs = all_tables()
     field = (shots, parts, freq_rows, trace_rows)
@@ -632,6 +712,9 @@
             pltpu.VMEM((TAPS + 2, freq_count * blocks, LANES), F32),
             pltpu.VMEM(table.shape, BF16),
             pltpu.VMEM((freq_rows, LANES), BF16),
+            pltpu.VMEM((max(detours, 1), parts, pack_rows, LANES), F32),
+            dma((max(detours, 1),)),
+            dma((max(detours, 1),)),
             dma,
             dma((shots,)),
             dma((shots,)),

time: 52.6 us -> 48.6 us (0.924)
  Pallas kernels: 48 us -> 44 us
    pallas_call x1, Pallas kernels: 48 us -> 44 us  [body(): pl.pallas_call(functools.partial(fit_kernel, weight, trace_count, freq_co...]
where the time goes in v3:
time: 48.6 us; the launch traced here: 48.5 us
  Pallas kernels  44 us (91%)
  local copies, waits for them, and re-layouts  3.84 us (8%)
  between operations  0.65 us (1%)
    pallas_call x1, Pallas kernels, body(): pl.pallas_call(functools.partial(fit_kernel, weight, trace_count, freq_co...  44 us
    unnamed x4, local copies, waits for them, and re-layouts  3.84 us

profile of v3, /device:TPU:0, one launch (start us, length us, event | category | flops | bytes accessed | tf_op | source)
XLA Modules:
  0.0 48.5 jit_solution(12037304579763647400)
XLA Ops:
  0.6 0.0 copy-start
  0.6 1.2 %copy-done = bf16[1920,256]{1,0:T(8,128)(2,1)S(1)} copy-done((bf16[1920,256]{1,0:T(8,128)(2,1)S(1)}, bf16[1920,256]{1,0:T(8,128)(2,1)}, u32[]{:S(2)}) %copy-start) | copy-done | bytes 983064
  1.8 44.0 %fit.1 = (f32[8,2,512,128]{3,2,1,0:T(8,128)S(1)}, f32[8,2,8,64]{3,2,1,0:T(8,128)S(1)}) custom-call(f32[8,2,512,128]{3,2,1,0:T(8,128)} %m_any.1, f32[8,2,512,128]{3,2,1,0:T(8,128)} %rec_any.1, bf16[1920,256]{1,0:T(8,128)(2,1)S(1)} %copy-done), custom_call_target="tpu_custom_call" | custom-call | tf_op jit(solution)/shard_map/fit/pallas_call | solution.py:689
  45.8 2.0 %copy.7 = f32[8,2,512,128]{3,2,1,0:T(8,128)} copy(f32[8,2,512,128]{3,2,1,0:T(8,128)S(1)} %get-tuple-element.4) | data formatting | bytes 8388608
  47.8 0.6 %copy.8 = f32[8,2,8,64]{3,2,1,0:T(8,128)} copy(f32[8,2,8,64]{3,2,1,0:T(8,128)S(1)} %get-tuple-element.5) | data formatting | bytes 65536
Async XLA Ops:
  0.6 1.2 %copy-start = (bf16[1920,256]{1,0:T(8,128)(2,1)S(1)}, bf16[1920,256]{1,0:T(8,128)(2,1)}, u32[]{:S(2)}) copy-start(bf16[1920,256]{1,0:T(8,128)(2,1)} %constant.2.clone.table_any) | copy-start | bytes 2949124

commit v4 on v3

--- a/solution.py
+++ b/solution.py
@@ -93,7 +93,7 @@
 
 
 def total_of(value):
-    return jnp.sum(jnp.sum(value, axis=1, keepdims=True), axis=0, keepdims=True)
+    return jnp.sum(jnp.sum(value, axis=0, keepdims=True), axis=1, keepdims=True)
 
 
 def column_sum(value):
@@ -249,38 +249,65 @@
     matrix[TAPS + 1] = jnp.where(is_real, -add_imag, exact(add_imag, back))
 
 
-def solve(weight, toep_real, toep_imag, gradient, matrix):
+def turn_matrix(matrix, square):
+    groups = LANES // matrix.shape[1]
+    run = TAPS // groups
+    for k in range(run):
+        square[k] = jnp.concatenate([matrix[g * run + k] for g in range(groups)], 0).T
+
+
+def solve(weight, toep_real, toep_imag, gradient, matrix, square, lags):
     blocks = gradient.shape[0]
-    lane = lanes_of((blocks, LANES))
-    is_real = lane < TAPS
+    groups = LANES // blocks
+    run = TAPS // groups
     toep_real = toep_real + matrix[TAPS]
     toep_imag = toep_imag + matrix[TAPS + 1]
-    for t in range(TAPS):
-        matrix[t] += jnp.where(is_real, turn(toep_real, t), turn(toep_imag, TAPS + t))
-
-    filters = jnp.zeros((blocks, LANES), F32)
+    for i, toep in enumerate((toep_real, toep_imag)):
+        base = jnp.concatenate([turn(toep, g * run) for g in range(groups)], 0).T
+        lags[i, :run] = base[LANES - run :]
+        lags[i, run:] = base[:TAPS]
+    for k in range(run):
+        square[k, :TAPS] += lags[0, run - k : run - k + TAPS]
+        square[k, TAPS:] += lags[1, run - k : run - k + TAPS]
+
+    shape = (LANES, LANES)
+    place = lanes_of(shape) % blocks
+    lane = lanes_of((run, LANES))
+
+    def grouped(rows):
+        result = rows[:run]
+        for g in range(1, groups):
+            result = jnp.where(lane >= g * blocks, rows[g * run : (g + 1) * run], result)
+        return result
+
+    gradient = jnp.concatenate([gradient] * groups, 0).T
+    filters = jnp.zeros(shape, F32)
     direction = norm_now = None
-    none = jnp.zeros((1, LANES), F32)
     for iteration in range(ITERS):
-        norm_next = total_of(gradient * gradient)
+        norm_next = total_of(gradient * gradient) * (1.0 / groups)
         if iteration == 0:
             direction = gradient
         else:
             direction = gradient + (norm_next / norm_now) * direction
         norm_now = norm_next
-        by_real = jnp.zeros((blocks, LANES), F32)
-        by_imag = jnp.zeros((blocks, LANES), F32)
-        for t in range(TAPS):
-            by_real = by_real + direction[:, t : t + 1] * matrix[t]
-            by_imag = by_imag + direction[:, TAPS + t : TAPS + t + 1] * matrix[t]
-        by_imag = turn(by_imag, TAPS)
-        normal = by_real + jnp.where(is_real, -by_imag, by_imag)
-        before = jnp.concatenate([none, direction[:-1]], 0)
-        after = jnp.concatenate([direction[1:], none], 0)
+        real, imag = grouped(direction[:TAPS]), grouped(direction[TAPS:])
+        by_real = jnp.zeros(shape, F32)
+        by_imag = jnp.zeros(shape, F32)
+        for k in range(run):
+            by_real = by_real + square[k] * real[k : k + 1]
+            by_imag = by_imag + square[k] * imag[k : k + 1]
+        normal = jnp.concatenate([by_real[:TAPS] - by_imag[TAPS:], by_real[TAPS:] + by_imag[:TAPS]], 0)
+        shift = LANES // 2
+        while shift >= blocks:
+            normal = normal + turn(normal, shift)
+            shift //= 2
+        before = jnp.where(place == 0, 0.0, turn(direction, 1))
+        after = jnp.where(place == blocks - 1, 0.0, turn(direction, -1))
         normal = normal + weight * (2.0 * direction - before - after)
-        step_len = norm_now / total_of(direction * normal)
+        step_len = norm_now / (total_of(direction * normal) * (1.0 / groups))
         filters = filters + step_len * direction
         gradient = gradient - step_len * normal
+    filters = filters.T[:blocks]
     rows = lax.broadcasted_iota(jnp.int32, (LANES, LANES), 0)
     columns = lanes_of((LANES, LANES))
     flip = (rows + columns == jnp.where(columns < TAPS, TAPS - 1, 3 * TAPS - 1)).astype(F32)
@@ -341,6 +368,8 @@
     taps,
     solved,
     matrix,
+    square,
+    lags,
     tables,
     ends_v,
     passing,
@@ -568,6 +597,7 @@
                 corner_all.at[other], corner_all.at[other], relay_send.at[o], relay_sem.at[other], freq=other
             ).wait_recv()
         prepare_corners(corner_all, matrix)
+        turn_matrix(matrix, square)
 
     def gather():
         whole = stats[me]
@@ -588,7 +618,7 @@
                 stats_all.at[other], stats_all.at[other], gather_send.at[o], gather_sem.at[other], freq=other
             ).wait_recv()
         rows = [stats_all[:, i].reshape(freq_count * blocks, LANES) for i in range(3)]
-        solved[...] = solve(weight, *rows, matrix).reshape(freq_count, blocks, LANES)
+        solved[...] = solve(weight, *rows, matrix, square, lags).reshape(freq_count, blocks, LANES)
         taps[me] = solved[layer]
         for o in range(1, trace_count):
             taps_copy(o).start()
@@ -680,6 +710,7 @@
     weight = 0.5 * FB * trace_rows * trace_count
     pack_rows = freq_rows * HALF // LANES
     detours = detour_count(shots, trace_count)
+    run = TAPS * freq_count * blocks // LANES
 
     table, runs = all_tables()
     field = (shots, parts, freq_rows, trace_rows)
@@ -710,6 +741,8 @@
             pltpu.VMEM((shots, blocks, LANES), F32),
             pltpu.VMEM((freq_count, blocks, LANES), F32),
             pltpu.VMEM((TAPS + 2, freq_count * blocks, LANES), F32),
+            pltpu.VMEM((run, LANES, LANES), F32),
+            pltpu.VMEM((2, run + TAPS, LANES), F32),
             pltpu.VMEM(table.shape, BF16),
             pltpu.VMEM((freq_rows, LANES), BF16),
             pltpu.VMEM((max(detours, 1), parts, pack_rows, LANES), F32),

time: 48.6 us -> 46.5 us (0.957)
  Pallas kernels: 44 us -> 41.9 us
    pallas_call x1, Pallas kernels: 44 us -> 41.9 us  [body(): pl.pallas_call(functools.partial(fit_kernel, weight, trace_count, freq_co...]
where the time goes in v4:
time: 46.5 us; the launch traced here: 46.4 us
  Pallas kernels  41.9 us (90%)
  local copies, waits for them, and re-layouts  3.84 us (8%)
  between operations  0.65 us (1%)
    pallas_call x1, Pallas kernels, body(): pl.pallas_call(functools.partial(fit_kernel, weight, trace_count, freq_co...  41.9 us
    unnamed x4, local copies, waits for them, and re-layouts  3.84 us

profile of v4, /device:TPU:0, one launch (start us, length us, event | category | flops | bytes accessed | tf_op | source)
XLA Modules:
  0.0 46.4 jit_solution(5669010726362145737)
XLA Ops:
  0.6 0.0 copy-start
  0.6 1.2 %copy-done = bf16[1920,256]{1,0:T(8,128)(2,1)S(1)} copy-done((bf16[1920,256]{1,0:T(8,128)(2,1)S(1)}, bf16[1920,256]{1,0:T(8,128)(2,1)}, u32[]{:S(2)}) %copy-start) | copy-done | bytes 983064
  1.8 41.9 %fit.1 = (f32[8,2,512,128]{3,2,1,0:T(8,128)S(1)}, f32[8,2,8,64]{3,2,1,0:T(8,128)S(1)}) custom-call(f32[8,2,512,128]{3,2,1,0:T(8,128)} %m_any.1, f32[8,2,512,128]{3,2,1,0:T(8,128)} %rec_any.1, bf16[1920,256]{1,0:T(8,128)(2,1)S(1)} %copy-done), custom_call_target="tpu_custom_call" | custom-call | tf_op jit(solution)/shard_map/fit/pallas_call | solution.py:720
  43.7 2.0 %copy.7 = f32[8,2,512,128]{3,2,1,0:T(8,128)} copy(f32[8,2,512,128]{3,2,1,0:T(8,128)S(1)} %get-tuple-element.4) | data formatting | bytes 8388608
  45.7 0.6 %copy.8 = f32[8,2,8,64]{3,2,1,0:T(8,128)} copy(f32[8,2,8,64]{3,2,1,0:T(8,128)S(1)} %get-tuple-element.5) | data formatting | bytes 65536
Async XLA Ops:
  0.6 1.2 %copy-start = (bf16[1920,256]{1,0:T(8,128)(2,1)S(1)}, bf16[1920,256]{1,0:T(8,128)(2,1)}, u32[]{:S(2)}) copy-start(bf16[1920,256]{1,0:T(8,128)(2,1)} %constant.2.clone.table_any) | copy-start | bytes 2949124

commit v5 on v4

--- a/solution.py
+++ b/solution.py
@@ -340,7 +340,7 @@
 
 
 def detour_count(shots, trace_count):
-    return (shots - 1) // 2 if trace_count >= 4 else 0
+    return max((shots - 2) // 2, 0) if trace_count >= 4 else 0
 
 
 def fit_kernel(
@@ -487,10 +487,10 @@
     def detoured(side, s):
         if not detours:
             return False
-        return (me == (middle - 1 if side == 0 else middle)) & (s > 0) & (lax.rem(s, 2) == 0)
+        return (me == (middle - 1 if side == 0 else middle)) & (s > 1) & (lax.rem(s, 2) == 1)
 
     def detour_copy(side, s):
-        i = jnp.maximum(s // 2 - 1, 0)
+        i = jnp.maximum(s - 3, 0) // 2
         return remote(
             edge.at[side, s],
             passing.at[i],
@@ -500,7 +500,7 @@
         )
 
     def pass_copy(side, i):
-        s = 2 * i + 2
+        s = 2 * i + 3
         return remote(
             passing.at[i],
             halo.at[side, s],
@@ -527,13 +527,19 @@
 
             @pl.when(passes[side])
             def _():
-                detour_copy(side, 2 * i + 2).wait_recv()
+                detour_copy(side, 2 * i + 3).wait_recv()
                 pass_copy(side, i).start()
 
+    def send_edges(s, carry):
+        local(m_any, m, m_sem, s).wait()
+        pack_edges(m, edge, s)
+        start_halo(s)
+        return carry
+
+    lax.fori_loop(0, shots, send_edges, 0)
     @pl.when((me == 0) | (me == last))
     def _():
         def send_corners(s, carry):
-            local(m_any, m, m_sem, s).wait()
             corners(m, ends_v, corner, s, me == last)
             for end, where in ends:
 
@@ -549,16 +555,6 @@
 
         lax.fori_loop(0, shots, send_corners, 0)
 
-    def send_edges(s, carry):
-        @pl.when((me > 0) & (me < last))
-        def _():
-            local(m_any, m, m_sem, s).wait()
-
-        pack_edges(m, edge, s)
-        start_halo(s)
-        return carry
-
-    lax.fori_loop(0, shots, send_edges, 0)
     for i in range(detours):
         pass_on(i)
 

time: 46.5 us -> 45.8 us (0.985)
  Pallas kernels: 41.9 us -> 41.2 us
    pallas_call x1, Pallas kernels: 41.9 us -> 41.2 us  [body(): pl.pallas_call(functools.partial(fit_kernel, weight, trace_count, freq_co...]
where the time goes in v5:
time: 45.8 us; the launch traced here: 45.6 us
  Pallas kernels  41.2 us (90%)
  local copies, waits for them, and re-layouts  3.84 us (8%)
  between operations  0.65 us (1%)
    pallas_call x1, Pallas kernels, body(): pl.pallas_call(functools.partial(fit_kernel, weight, trace_count, freq_co...  41.2 us
    unnamed x4, local copies, waits for them, and re-layouts  3.84 us

profile of v5, /device:TPU:0, one launch (start us, length us, event | category | flops | bytes accessed | tf_op | source)
XLA Modules:
  0.0 45.6 jit_solution(13932897501324910292)
XLA Ops:
  0.6 0.0 copy-start
  0.6 1.2 %copy-done = bf16[1920,256]{1,0:T(8,128)(2,1)S(1)} copy-done((bf16[1920,256]{1,0:T(8,128)(2,1)S(1)}, bf16[1920,256]{1,0:T(8,128)(2,1)}, u32[]{:S(2)}) %copy-start) | copy-done | bytes 983064
  1.8 41.2 %fit.1 = (f32[8,2,512,128]{3,2,1,0:T(8,128)S(1)}, f32[8,2,8,64]{3,2,1,0:T(8,128)S(1)}) custom-call(f32[8,2,512,128]{3,2,1,0:T(8,128)} %m_any.1, f32[8,2,512,128]{3,2,1,0:T(8,128)} %rec_any.1, bf16[1920,256]{1,0:T(8,128)(2,1)S(1)} %copy-done), custom_call_target="tpu_custom_call" | custom-call | tf_op jit(solution)/shard_map/fit/pallas_call | solution.py:716
  43.0 2.0 %copy.7 = f32[8,2,512,128]{3,2,1,0:T(8,128)} copy(f32[8,2,512,128]{3,2,1,0:T(8,128)S(1)} %get-tuple-element.4) | data formatting | bytes 8388608
  45.0 0.6 %copy.8 = f32[8,2,8,64]{3,2,1,0:T(8,128)} copy(f32[8,2,8,64]{3,2,1,0:T(8,128)S(1)} %get-tuple-element.5) | data formatting | bytes 65536
Async XLA Ops:
  0.6 1.2 %copy-start = (bf16[1920,256]{1,0:T(8,128)(2,1)S(1)}, bf16[1920,256]{1,0:T(8,128)(2,1)}, u32[]{:S(2)}) copy-start(bf16[1920,256]{1,0:T(8,128)(2,1)} %constant.2.clone.table_any) | copy-start | bytes 2949124
